TPU v7x, 32 devices: a whole 2x2x4 slice. The times are simulated.
32 devices in a mesh: seq: 8 (over z, y), grp: 4 (over x, core).
Axes of the slice: x: 2, y: 2, z: 4, core: 2. Of those that a mesh axis runs over, the one named last changes fastest.
Arguments:
- event_codes: int32 [262144], P(('seq', 'grp')), may hold values from 0 to 255
- window_ends: int32 [24576], P(('seq', 'grp')), may hold values from 0 to 8191, as said below
- window_count: int32 [32], P(('seq', 'grp')), may hold values from 1 to 768, as said below
- handed: int32 [32], P(('seq', 'grp')), may hold values from 0 to 256, as said below
Outputs:
- window_share: float32 [16384, 256], P(('seq', 'grp'))
- share_gap: float32 [16384, 256], P(('seq', 'grp'))
Inputs may be any that keep to these rules, and one draw needn't show every extreme that they name: `window_ends`: for each shard, its first window_count slots hold distinct offsets in rising order; the remaining slots hold 0. `window_count`: some shard has 768 windows in every draw. `handed`: at most the shard's window_count minus 1; 0 on the last shard of each group along grp; the windows a shard keeps plus those it receives number at most 512, and exactly 512 on some shard that passes 512 // 2 in every draw.
All inputs are finite; a program needn't handle non-finite values.
Results may differ from a plain program's by a relative error of at most 0.0003.
Values sent between devices are 32-bit elements; how exact they have to be, the bound alone decides.
No kernel may reach another device: no remote copies, remote signals or barrier semaphores. Data moves between devices by JAX's collectives and lax.ppermute only.
A program may use at most 64 MiB of HBM per device.

v0:
```python
import jax
import jax.numpy as jnp
from jax import lax
from jax.sharding import PartitionSpec as P

CODES = 256
WINDOW = 4096


def entering(shard, axis, combine, identity):
    size, position = (lax.axis_size(axis), lax.axis_index(axis))
    everything = lax.all_gather(shard, axis)
    start = jnp.broadcast_to(jnp.asarray(identity, shard.dtype), shard.shape)

    def hop(k, before):
        reached = k < position
        new = combine(before, everything[k])
        return jnp.where(reached, new, before)

    return lax.fori_loop(0, size, hop, start)


def from_behind(block, axis, distance):
    devices = range(lax.axis_size(axis))
    route = [(i - distance, i) for i in devices if i - distance in devices]
    return lax.ppermute(block, axis, route)


def event_counts(marks, points, block_len, label_shift):
    portions = marks.reshape(marks.shape[0] // block_len, block_len)
    anchors = jnp.arange(portions.shape[0], dtype=jnp.int32) * block_len
    labels = jnp.arange(CODES, dtype=jnp.int32) + label_shift
    offsets = jnp.arange(block_len, dtype=jnp.int32)

    def advance(total, inputs):
        portion, anchor = inputs
        onehot = (portion[:, None] == labels[None, :]).astype(jnp.bfloat16)
        before = ((anchor + offsets)[None, :] <= points[:, None]).astype(jnp.bfloat16)
        return (total + jnp.dot(before, onehot, preferred_element_type=jnp.float32), None)

    initial = jnp.zeros((points.shape[0], CODES), jnp.float32)
    return lax.scan(advance, initial, (portions, anchors))[0]


def add_rows(earlier, later):
    return earlier + later


def local(event_codes, window_ends, window_count, handed):
    shard_len = event_codes.shape[0]
    slot_total = window_ends.shape[0]
    out_rows = 2 * slot_total // 3
    handoff_rows = out_rows // 2
    block_len = min(512, shard_len)
    shard_index = lax.axis_index(("seq", "grp"))
    totals = event_counts(event_codes, jnp.full((1,), shard_len - 1, jnp.int32), block_len, 0)[0]
    offset = entering(totals, ("seq", "grp"), add_rows, jnp.zeros_like(totals))
    starts = window_ends - WINDOW
    own_tally = event_counts(event_codes, jnp.concatenate([window_ends, starts]), block_len, 0)
    end_tally = own_tally[:slot_total]
    start_tally = own_tally[slot_total:]
    inside = (starts >= 0)[:, None]
    tail_marks = from_behind(event_codes[shard_len - WINDOW :] + 1, ("seq", "grp"), 1)
    tail_points = jnp.concatenate([window_ends, jnp.full((1,), WINDOW - 1, jnp.int32)])
    tail_tally = event_counts(tail_marks, tail_points, min(512, WINDOW), 1)
    after_start = tail_tally[slot_total:] - tail_tally[:slot_total]
    window_tally = jnp.where(inside, end_tally - start_tally, end_tally + after_start)
    running = offset[None, :] + end_tally
    end_position = shard_index * shard_len + window_ends
    length = jnp.minimum(WINDOW, end_position + 1).astype(jnp.float32)
    share_rows = CODES * window_tally / length[:, None]
    gap_rows = share_rows - CODES * running / (end_position + 1).astype(jnp.float32)[:, None]
    kept_count = window_count[0] - handed[0]
    sent_ids = jnp.arange(handoff_rows, dtype=jnp.int32)
    source = jnp.clip(kept_count + sent_ids, 0, slot_total - 1)
    sending = (sent_ids < handed[0])[:, None]
    outgoing = (
        jnp.where(sending, share_rows[source], 0.0),
        jnp.where(sending, gap_rows[source], 0.0),
        handed.astype(jnp.float32),
    )
    got_share, got_gap, got_count = from_behind((outgoing[0], outgoing[1], outgoing[2]), "grp", 1)
    arrived = got_count[0].astype(jnp.int32)
    row_ids = jnp.arange(out_rows, dtype=jnp.int32)
    from_prior = (row_ids < arrived)[:, None]
    prior_slot = jnp.clip(row_ids, 0, handoff_rows - 1)
    own_slot = jnp.clip(row_ids - arrived, 0, slot_total - 1)
    own_valid = ((row_ids >= arrived) & (row_ids - arrived < kept_count))[:, None]
    window_share = jnp.where(
        from_prior, got_share[prior_slot], jnp.where(own_valid, share_rows[own_slot], 0.0)
    )
    share_gap = jnp.where(
        from_prior, got_gap[prior_slot], jnp.where(own_valid, gap_rows[own_slot], 0.0)
    )
    return (window_share, share_gap)


def solution(mesh):
    in_specs = (P(("seq", "grp")), P(("seq", "grp")), P(("seq", "grp")), P(("seq", "grp")))
    out_specs = (P(("seq", "grp"), None), P(("seq", "grp"), None))
    return jax.shard_map(local, mesh=mesh, in_specs=in_specs, out_specs=out_specs, check_vma=False)
```

profile of v0, /device:TPU:0, one launch (start us, length us, event | category | flops | bytes accessed | tf_op | source)
XLA Modules:
  0.0 156.9 jit_solution(14326714553366858153)
XLA Ops:
  1.4 2.4 %collective-permute-start.1 = (s32[4096]{0:T(1024)S(1)}, s32[4096]{0:T(1024)S(1)}, u32[]{:S(2)}, u32[]{:S(2)}) collective-permute-start(s32[4096]{0:T(1024)S(1)} %slice_add_fusion), channel_id=1, source_target_pairs={{0,1},{1,2},{2,3},{3,4},{4,5},{5,6},{6,7},{7,8},{8,9},{9,10},{10,1... | collective-permute-start | bytes 49160 | tf_op jit(solution)/shard_map/ppermute | solution.py:26
  4.4 5.4 %collective-permute-start = (f32[1]{0:T(128)}, f32[1]{0:T(128)}, u32[]{:S(2)}, u32[]{:S(2)}) collective-permute-start(f32[1]{0:T(128)} %convert_element_type.21), channel_id=1, source_target_pairs={{0,1},{1,2},{2,3},{4,5},{5,6},{6,7},{8,9},{9,10},{10,11},{12,13},{... | collective-permute-start | bytes 20 | tf_op jit(solution)/shard_map/ppermute | solution.py:26
  12.7 43.0 %while.47 = (s32[]{:T(128)}, f32[1536,256]{1,0:T(8,128)S(1)}, s32[16]{0:T(128)S(1)}, s32[1536]{0:T(1024)S(1)}, s32[16,512]{1,0:T(8,128)S(1)}, /*index=5*/s32[]{:T(128)}, s32[]{:T(128)}) while((s32[]{:T(128)}, f32[1536,256]{1,0:T(8,128)S(1)}, s32[16]{0:T(128)S(1)}, s32[1536]{0:T(1024)S(1)}, s32[16,512]{1,0:T(8,128)S(1)}, ...), condition=%wide.region_1.2_spmd.clone, body=%wide.region_0.1_spmd.clone.sunk | while | flops 404357632 | bytes 3162219 | solution.py:42
  14.1 1.3 fusion.43
  16.8 1.3 fusion.43
  22.2 1.3 fusion.43
  24.9 1.3 fusion.43
  30.3 1.3 fusion.43
  35.7 1.3 fusion.43
  38.3 1.3 fusion.43
  43.7 1.3 fusion.43
  49.1 1.3 fusion.43
  51.8 1.3 fusion.43
  55.8 24.8 %while.49 = (s32[]{:T(128)}, f32[1,256]{1,0:T(1,128)S(1)}, s32[16]{0:T(128)S(1)}, s32[16,512]{1,0:T(8,128)S(1)}, s32[]{:T(128)}, /*index=5*/s32[]{:T(128)}) while((s32[]{:T(128)}, f32[1,256]{1,0:T(1,128)S(1)}, s32[16]{0:T(128)S(1)}, s32[16,512]{1,0:T(8,128)S(1)}, s32[]{:T(128)}, /*index=5*/s32[]{:T(128)}) %tuple.107), condition=%wide.region_5.6_spmd.clone, body=%wide.region_4.5_spmd.clone.sunk | while | flops 394755 | bytes 10339 | solution.py:42
  80.6 40.3 %all-gather = f32[32,1,256]{2,1,0:T(1,128)S(1)} all-gather(f32[1,1,256]{2,1,0:T(1,128)S(1)} %bitcast.47), channel_id=1, replica_groups=mesh['seq'=8,'grp'=4] {'seq','grp'}, dimensions={0}, use_global_device_ids=true | all-gather | bytes 33792 | tf_op jit(solution)/shard_map/all_gather | solution.py:12
  120.9 1.7 %while.50 = (s32[]{:T(128)}, f32[256]{0:T(256)S(1)}, s32[]{:T(128)}, f32[32,256]{1,0:T(8,128)S(1)}, s32[]{:T(128)}, /*index=5*/s32[]{:T(128)}) while((s32[]{:T(128)}, f32[256]{0:T(256)S(1)}, s32[]{:T(128)}, f32[32,256]{1,0:T(8,128)S(1)}, s32[]{:T(128)}, /*index=5*/s32[]{:T(128)}) %tuple.106), condition=%wide.region_7.8_spmd.clone, body=%wide.region_6.7_spmd.clone.sunk | while | flops 772 | bytes 5213 | solution.py:20
  124.0 16.0 %while.48 = (s32[]{:T(128)}, f32[769,256]{1,0:T(8,128)S(1)}, s32[8]{0:T(128)S(1)}, s32[769]{0:T(1024)S(1)}, s32[8,512]{1,0:T(8,128)S(1)}, /*index=5*/s32[]{:T(128)}, s32[]{:T(128)}) while((s32[]{:T(128)}, f32[769,256]{1,0:T(8,128)S(1)}, s32[8]{0:T(128)S(1)}, s32[769]{0:T(1024)S(1)}, s32[8,512]{1,0:T(8,128)S(1)}, ...), condition=%wide.region_3.4_spmd.clone, body=%wide.region_2.3_spmd.clone.sunk | while | flops 202508032 | bytes 1590383 | solution.py:42
  140.9 1.5 divide_subtract_fusion
  145.2 2.2 %collective-permute-start.2 = (f32[256,256]{1,0:T(8,128)}, f32[256,256]{1,0:T(8,128)S(1)}, u32[]{:S(2)}, u32[]{:S(2)}) collective-permute-start(f32[256,256]{1,0:T(8,128)} %get-tuple-element.313), channel_id=1, source_target_pairs={{0,1},{1,2},{2,3},{4,5},{5,6},{6,7},{8,9},{9,10},{10,11},{12,13},{... | collective-permute-start | bytes 786440 | tf_op jit(solution)/shard_map/ppermute | solution.py:26
  147.4 1.9 %collective-permute-start.3 = (f32[256,256]{1,0:T(8,128)S(1)}, f32[256,256]{1,0:T(8,128)S(1)}, u32[]{:S(2)}, u32[]{:S(2)}) collective-permute-start(f32[256,256]{1,0:T(8,128)S(1)} %get-tuple-element.312), channel_id=1, source_target_pairs={{0,1},{1,2},{2,3},{4,5},{5,6},{6,7},{8,9},{9,10},{10,11},{12,13},{... | collective-permute-start | bytes 786440 | tf_op jit(solution)/shard_map/ppermute | solution.py:26
  149.4 1.6 %gather_fusion.2 = f32[512,256]{1,0:T(8,128)S(1)} fusion(f32[768,256]{1,0:T(8,128)S(1)} %get-tuple-element.306, s32[1024]{0:T(1024)S(1)} %pad_clamp_fusion), kind=kCustom, calls=%fused_computation.2 | custom fusion | bytes 1050624 | tf_op jit(solution)/shard_map/gather | solution.py:90
  151.0 1.6 %gather_fusion.5 = f32[512,256]{1,0:T(8,128)S(1)} fusion(f32[768,256]{1,0:T(8,128)S(1)} %get-tuple-element.305, s32[1024]{0:T(1024)S(1)} %pad_clamp_fusion), kind=kCustom, calls=%fused_computation.5 | custom fusion | bytes 1050624 | tf_op jit(solution)/shard_map/gather | solution.py:93
  152.6 1.6 %gather_fusion.1 = f32[512,256]{1,0:T(8,128)S(1)} fusion(f32[256,256]{1,0:T(8,128)S(1)} %collective-permute-done.2, s32[1024]{0:T(1024)S(1)} %pad_clamp_fusion.1), kind=kCustom, calls=%fused_computation.1 | custom fusion | bytes 1050624 | tf_op jit(solution)/shard_map/gather | solution.py:90
  154.2 1.6 %gather_fusion.4 = f32[512,256]{1,0:T(8,128)S(1)} fusion(f32[256,256]{1,0:T(8,128)S(1)} %collective-permute-done.3, s32[1024]{0:T(1024)S(1)} %pad_clamp_fusion.1), kind=kCustom, calls=%fused_computation.4 | custom fusion | bytes 1050624 | tf_op jit(solution)/shard_map/gather | solution.py:93
  (273 shorter events, 78.7 us)
Async XLA Ops:
  1.4 122.6 %collective-permute-start.1 = (s32[4096]{0:T(1024)S(1)}, s32[4096]{0:T(1024)S(1)}, u32[]{:S(2)}, u32[]{:S(2)}) collective-permute-start(s32[4096]{0:T(1024)S(1)} %slice_add_fusion), channel_id=1, source_target_pairs={{0,1},{1,2},{2,3},{3,4},{4,5},{5,6},{6,7},{7,8},{8,9},{9,10},{10,1... | collective-permute-start | bytes 49160 | tf_op jit(solution)/shard_map/ppermute | solution.py:26
  4.4 118.9 %collective-permute-start = (f32[1]{0:T(128)}, f32[1]{0:T(128)}, u32[]{:S(2)}, u32[]{:S(2)}) collective-permute-start(f32[1]{0:T(128)} %convert_element_type.21), channel_id=1, source_target_pairs={{0,1},{1,2},{2,3},{4,5},{5,6},{6,7},{8,9},{9,10},{10,11},{12,13},{... | collective-permute-start | bytes 20 | tf_op jit(solution)/shard_map/ppermute | solution.py:26
  12.7 109.9 %copy-start.1 = (s32[768]{0:T(1024)S(1)}, s32[768]{0:T(1024)}, u32[]{:S(2)}) copy-start(s32[768]{0:T(1024)} %param.13) | copy-start | bytes 9220
  140.0 0.9 copy-start
  145.2 7.4 %collective-permute-start.2 = (f32[256,256]{1,0:T(8,128)}, f32[256,256]{1,0:T(8,128)S(1)}, u32[]{:S(2)}, u32[]{:S(2)}) collective-permute-start(f32[256,256]{1,0:T(8,128)} %get-tuple-element.313), channel_id=1, source_target_pairs={{0,1},{1,2},{2,3},{4,5},{5,6},{6,7},{8,9},{9,10},{10,11},{12,13},{... | collective-permute-start | bytes 786440 | tf_op jit(solution)/shard_map/ppermute | solution.py:26
  147.4 6.7 %collective-permute-start.3 = (f32[256,256]{1,0:T(8,128)S(1)}, f32[256,256]{1,0:T(8,128)S(1)}, u32[]{:S(2)}, u32[]{:S(2)}) collective-permute-start(f32[256,256]{1,0:T(8,128)S(1)} %get-tuple-element.312), channel_id=1, source_target_pairs={{0,1},{1,2},{2,3},{4,5},{5,6},{6,7},{8,9},{9,10},{10,11},{12,13},{... | collective-permute-start | bytes 786440 | tf_op jit(solution)/shard_map/ppermute | solution.py:26
where the time goes:
time: 158 us; the launch traced here: 157 us
  blocking collectives  40.3 us (26%)
  local copies, waits for them, and re-layouts  35.8 us (23%)
  other arithmetic  33.3 us (21%)
  matrix products  30.2 us (19%)
  starting transfers between devices  12 us (8%)
  between operations  2.83 us (2%)
  loops' own time  2.47 us (2%)
    all_gather x1, blocking collectives, entering(): everything = lax.all_gather(shard, axis)  40.3 us
    dot_general x40, matrix products, advance(): jnp.dot(before, onehot, preferred_element_type=jnp.float32)  30.2 us
    dynamic_slice x80, local copies, waits for them, and re-layouts, event_counts(): return lax.scan(advance, initial, (portions, anchors))[0]  25.5 us
    add x24, other arithmetic, advance(): anchor + offsets  16.1 us
    ppermute x4, starting transfers between devices, from_behind(): return lax.ppermute(block, axis, route)  12 us
    le x16, other arithmetic, advance(): (anchor + offsets)[None, :] <= points[:, None]  10.4 us
  transfers between devices with their start and end apart: 4, of which 0 were waited for; matrix products, arithmetic and copies ran while one was open for 48% of the time, Pallas kernels for 0%

commit v1 on v0

v1 whole, which is shorter than its diff:
```python
import jax
import jax.numpy as jnp
from jax import lax
from jax.experimental import pallas as pl
from jax.experimental.pallas import tpu as pltpu
from jax.sharding import PartitionSpec as P

CODES = 256
WINDOW = 4096
LANES = 128
BLOCK = 16
PACK = 16
AXES = ("seq", "grp")
F32 = jnp.float32
BF16 = jnp.bfloat16


def label_groups():
    base = lax.broadcasted_iota(jnp.int32, (PACK, LANES), 0).astype(F32)
    return [(base + PACK * k).astype(BF16) for k in range(CODES // PACK)]


def tally_rows(rows, labels):
    total = [None] * len(labels)
    one, zero = jnp.ones((PACK, LANES), BF16), jnp.zeros((PACK, LANES), BF16)
    for row in rows:
        wide = jnp.broadcast_to(row, (PACK, LANES)).astype(BF16)
        for k, label in enumerate(labels):
            hit = jnp.where(wide == label, one, zero)
            total[k] = hit if total[k] is None else total[k] + hit
    return total


def first_kernel(place, counts, codes, ends, out_totals, out_pack, tally):
    devices = out_totals.shape[0]
    rows = codes.shape[0]
    slots = ends.shape[1]
    values = codes[...]
    out_pack[:rows, :] = values
    held, handed = counts[0], counts[1]
    start = held - handed
    shifted = pltpu.roll(
        jnp.broadcast_to(ends[...], (8, slots)), lax.rem(slots - start, slots), axis=1
    )
    passed = (slots // 3) // LANES
    for k in range(passed):
        out_pack[rows + k : rows + k + 1, :] = shifted[:1, k * LANES : (k + 1) * LANES]
    out_pack[rows + passed : rows + passed + 1, :] = jnp.full((1, LANES), handed, jnp.int32)
    rest = out_pack.shape[0] - rows - passed - 1
    out_pack[rows + passed + 1 :, :] = jnp.zeros((rest, LANES), jnp.int32)
    wide = values.astype(F32)
    groups = tally_rows([wide[r : r + 1, :] for r in range(rows)], label_groups())
    for k, group in enumerate(groups):
        tally[k * PACK : (k + 1) * PACK, :] = group
    total = lax.dot_general(
        jnp.ones((8, LANES), BF16),
        tally[...],
        (((1,), (1,)), ((), ())),
        preferred_element_type=F32,
    )
    out_totals[...] = jnp.broadcast_to(total[:1, :].reshape(1, 1, CODES), (devices, 1, CODES))


def main_kernel(place, counts, codes, ends, pack, tail, out_share, out_base, out_weight,
                turned, side, left, mask, parts):
    shard, within = place[0], place[1]
    held, handed = counts[0], counts[1]
    rows = codes.shape[0]
    slots = ends.shape[1]
    tail_rows = tail.shape[0]
    shard_len = rows * LANES
    out_rows = out_share.shape[0]
    passed = (slots // 3) // LANES
    groups = LANES // BLOCK
    side_blocks = side.shape[0] // BLOCK
    split = LANES // tail_rows
    labels = label_groups()

    before = jnp.where(shard > 0, pack[:rows, :], -1)
    turned[...] = jnp.concatenate([before, codes[...]], axis=0).astype(F32).T
    far = jnp.where(shard > 1, tail[...], -1).astype(F32)
    step = LANES // split
    stacked = jnp.concatenate(
        [far] + [pltpu.roll(far, LANES - step * k, axis=1) for k in range(1, split)], axis=0
    )
    side[...] = stacked.T[:step, :]

    for g in range(groups):
        found = tally_rows([turned[g * BLOCK + i : g * BLOCK + i + 1, :] for i in range(BLOCK)], labels)
        for k, group in enumerate(found):
            left[k * PACK : (k + 1) * PACK, g * LANES : (g + 1) * LANES] = group
    for g in range(side_blocks):
        found = tally_rows([side[g * BLOCK + i : g * BLOCK + i + 1, :] for i in range(BLOCK)], labels)
        column = (groups + g) * LANES
        for k, group in enumerate(found):
            left[k * PACK : (k + 1) * PACK, column : column + LANES] = group
    for g in range(groups):
        here = turned[g * BLOCK : (g + 1) * BLOCK, :]
        if g + 1 < groups:
            after = turned[(g + 1) * BLOCK : (g + 2) * BLOCK, :]
        else:
            after = pltpu.roll(turned[:BLOCK, :], LANES - 1, axis=1)
        left[CODES:, g * LANES : (g + 1) * LANES] = (after - here).astype(BF16)
    lane = lax.broadcasted_iota(jnp.int32, (BLOCK, LANES), 1)
    for g in range(side_blocks):
        here = side[g * BLOCK : (g + 1) * BLOCK, :]
        if g + 1 < side_blocks:
            after = side[(g + 1) * BLOCK : (g + 2) * BLOCK, :]
        else:
            top = side[:BLOCK, :]
            after = jnp.where(
                lane < LANES - tail_rows,
                pltpu.roll(top, LANES - tail_rows, axis=1),
                pltpu.roll(top, LANES - tail_rows - 1, axis=1),
            )
            after = jnp.where(lane < LANES - 1, after, turned[:BLOCK, :1])
        column = (groups + g) * LANES
        left[CODES:, column : column + LANES] = (after - here).astype(BF16)

    got = jnp.max(pack[rows + passed : rows + passed + 1, :])
    arrived = jnp.where(within > 0, got, 0)
    own = pltpu.roll(jnp.broadcast_to(ends[...], (8, slots)), arrived, axis=1)[:1, :out_rows]
    sent = [pack[rows + k : rows + k + 1, :] for k in range(passed)]
    sent = jnp.concatenate(sent + [jnp.zeros((1, out_rows - passed * LANES), jnp.int32)], axis=1)
    row = lax.broadcasted_iota(jnp.int32, (1, out_rows), 1)
    end = jnp.where(row < arrived, sent - shard_len, own)
    valid = row < arrived + held - handed
    end = jnp.where(valid, end, 0)

    upper = end + 1 + shard_len
    lower = upper - WINDOW
    upper_block, lower_block = upper >> 4, lower >> 4
    down = lax.broadcasted_iota(jnp.int32, (PACK, out_rows), 0).astype(F32)
    downs = [(down + PACK * k).astype(BF16) for k in range(LANES // PACK)]
    one, zero = jnp.ones((PACK, out_rows), BF16), jnp.zeros((PACK, out_rows), BF16)

    def limit(value):
        bound = jnp.clip(value, 0, LANES).astype(F32)
        return jnp.broadcast_to(bound, (PACK, out_rows)).astype(BF16)

    for g in range(groups):
        high = limit((upper_block - g + groups - 1) >> 3)
        low = limit((lower_block - g + groups - 1) >> 3)
        for k in range(LANES // PACK):
            reach = jnp.where(downs[k] < high, one, zero)
            skip = jnp.where(downs[k] < low, one, zero)
            first = g * LANES + k * PACK
            mask[first : first + PACK, :out_rows] = reach - one if k * PACK < rows else reach
            mask[first : first + PACK, out_rows:] = reach - skip
    side_block = lower_block + tail_rows * groups
    for g in range(side_blocks):
        for part in range(split):
            low = limit((side_block - side_blocks * part - g + groups - 1) >> 3)
            for k in range(tail_rows // PACK):
                first = (groups + g) * LANES + part * tail_rows + k * PACK
                mask[first : first + PACK, out_rows:] = jnp.where(downs[k] < low, zero, one)

    main_depth = groups * LANES
    parts[:, :out_rows] = jnp.dot(
        left[:, :main_depth], mask[:main_depth, :out_rows], preferred_element_type=F32
    )
    parts[:, out_rows:] = jnp.dot(left[...], mask[:, out_rows:], preferred_element_type=F32)

    upper_codes = parts[CODES:, :out_rows] + turned[:BLOCK, rows : rows + 1]
    lower_codes = upper_codes - parts[CODES:, out_rows:]
    inner = lax.broadcasted_iota(jnp.int32, (BLOCK, out_rows), 0)
    upper_codes = jnp.where(inner < (upper & (BLOCK - 1)), upper_codes, -2.0)
    lower_codes = jnp.where(inner < (lower & (BLOCK - 1)), lower_codes, -2.0)
    position = (shard * shard_len + end + 1).astype(F32)
    share_weight = jnp.where(valid, CODES / jnp.minimum(position, float(WINDOW)), 0.0)
    gap_weight = jnp.where(valid, CODES / position, 0.0)
    for q in range(out_rows // LANES):
        cut = slice(q * LANES, (q + 1) * LANES)
        ups = tally_rows([upper_codes[i : i + 1, cut] for i in range(BLOCK)], labels)
        lows = tally_rows([lower_codes[i : i + 1, cut] for i in range(BLOCK)], labels)
        lower_cut = slice(out_rows + q * LANES, out_rows + (q + 1) * LANES)
        shares, bases = [], []
        for k in range(CODES // PACK):
            span = slice(k * PACK, (k + 1) * PACK)
            up = ups[k].astype(F32)
            run = parts[span, cut] + up
            tally = parts[span, lower_cut] + (up - lows[k].astype(F32))
            share = tally * share_weight[:, cut]
            shares.append(share)
            bases.append(share - run * gap_weight[:, cut])
        out_share[cut, :] = jnp.concatenate(shares, axis=0).T
        out_base[cut, :] = jnp.concatenate(bases, axis=0).T
        out_weight[cut, :] = jnp.broadcast_to(gap_weight[:, cut], (LANES, LANES)).T


def last_kernel(place, totals, base, weight, out_gap):
    devices = totals.shape[0]
    order = lax.broadcasted_iota(jnp.int32, (devices, 1, CODES), 0)
    offset = jnp.sum(jnp.where(order < place[0], totals[...], 0.0), axis=0)
    for k in range(CODES // LANES):
        cut = slice(k * LANES, (k + 1) * LANES)
        out_gap[:, cut] = base[:, cut] - weight[...] * offset[:, cut]


def local(event_codes, window_ends, window_count, handed):
    seq, grp = lax.axis_size("seq"), lax.axis_size("grp")
    devices = seq * grp
    shard_len, slots = event_codes.shape[0], window_ends.shape[0]
    rows = shard_len // LANES
    tail_rows = WINDOW // LANES
    out_rows = 2 * slots // 3
    passed = (slots // 3) // LANES
    pack_rows = -(-(rows + passed + 1) // 8) * 8
    within = lax.axis_index("grp")
    place = jnp.stack([lax.axis_index("seq") * grp + within, within]).astype(jnp.int32)
    counts = jnp.concatenate([window_count, handed])
    codes = event_codes.reshape(rows, LANES)
    ends = window_ends.reshape(1, slots)
    smem = pl.BlockSpec(memory_space=pltpu.SMEM)
    vmem = pl.BlockSpec(memory_space=pltpu.VMEM)

    totals, pack = pl.pallas_call(
        first_kernel,
        out_shape=(
            jax.ShapeDtypeStruct((devices, 1, CODES), F32),
            jax.ShapeDtypeStruct((pack_rows, LANES), jnp.int32),
        ),
        in_specs=[smem, smem, vmem, vmem],
        out_specs=(vmem, vmem),
        scratch_shapes=[pltpu.VMEM((CODES, LANES), BF16)],
        name="totals",
    )(place, counts, codes, ends)
    everyone = lax.all_to_all(totals, AXES, 0, 0, tiled=True)
    next_one = [(i, i + 1) for i in range(devices - 1)]
    next_two = [(i, i + 2) for i in range(devices - 2)]
    got_pack = lax.ppermute(pack, AXES, next_one)
    got_tail = lax.ppermute(codes[rows - tail_rows :], AXES, next_two)

    groups = LANES // BLOCK
    split = LANES // tail_rows
    depth = (rows + rows) * LANES // BLOCK + tail_rows * LANES // BLOCK
    share, base, weight = pl.pallas_call(
        main_kernel,
        out_shape=(
            jax.ShapeDtypeStruct((out_rows, CODES), F32),
            jax.ShapeDtypeStruct((out_rows, CODES), F32),
            jax.ShapeDtypeStruct((out_rows, LANES), F32),
        ),
        in_specs=[smem, smem, vmem, vmem, vmem, vmem],
        out_specs=(vmem, vmem, vmem),
        scratch_shapes=[
            pltpu.VMEM((LANES, LANES), F32),
            pltpu.VMEM((LANES // split, LANES), F32),
            pltpu.VMEM((CODES + BLOCK, depth), BF16),
            pltpu.VMEM((depth, 2 * out_rows), BF16),
            pltpu.VMEM((CODES + BLOCK, 2 * out_rows), F32),
        ],
        cost_estimate=pl.CostEstimate(
            flops=2 * (CODES + BLOCK) * depth * 2 * out_rows, bytes_accessed=2**21, transcendentals=0
        ),
        name="windows",
    )(place, counts, codes, ends, got_pack, got_tail)
    gap = pl.pallas_call(
        last_kernel,
        out_shape=jax.ShapeDtypeStruct((out_rows, CODES), F32),
        in_specs=[smem, vmem, vmem, vmem],
        out_specs=vmem,
        name="gap",
    )(place, everyone, base, weight)
    return share, gap


def solution(mesh):
    in_specs = (P(AXES), P(AXES), P(AXES), P(AXES))
    out_specs = (P(AXES, None), P(AXES, None))
    return jax.shard_map(local, mesh=mesh, in_specs=in_specs, out_specs=out_specs, check_vma=False)
```

time: 158 us -> 28.2 us (0.18)
  blocking collectives: 40.3 us -> 0 us
  local copies, waits for them, and re-layouts: 35.8 us -> 2.42 us
  other arithmetic: 33.3 us -> 0.66 us
  matrix products: 30.2 us -> 0 us
  Pallas kernels: 0 us -> 8.87 us
  loops' own time: 2.47 us -> 0 us
    all_gather x1 -> x0, blocking collectives: 40.3 us -> none  [entering(): everything = lax.all_gather(shard, axis)]
    dot_general x40 -> x0, matrix products: 30.2 us -> none  [advance(): jnp.dot(before, onehot, preferred_element_type=jnp.float32)]
    dynamic_slice x112 -> x0, local copies, waits for them, and re-layouts: 25.8 us -> none  [the longest x80 25.5 us: event_counts(): return lax.scan(advance, initial, (portions, anchors))[0]]
    add x33 -> x0, other arithmetic: 16.9 us -> none  [the longest x24 16.1 us: advance(): anchor + offsets]
    le x16 -> x0, other arithmetic: 10.4 us -> none  [advance(): (anchor + offsets)[None, :] <= points[:, None]]
    pallas_call x0 -> x3, Pallas kernels: none -> 8.87 us  [the longest x1 4.86 us: local(): pl.pallas_call(main_kernel, out_shape=(jax.ShapeDtypeStruct((out_rows, CO...]
    gather x6 -> x0, local copies, waits for them, and re-layouts: 8.23 us -> none  [the longest x1 1.57 us: local(): share_rows[own_slot]]
    all_to_all x0 -> x1, starting transfers between devices: none -> 5.82 us  [local(): everyone = lax.all_to_all(totals, AXES, 0, 0, tiled=True)]
  transfers between devices with their start and end apart: 4 -> 3, of which waited for: 0 -> 1; matrix products, arithmetic and copies ran while one was open for 48% -> 0% of each run, Pallas kernels for 0% -> 18%
where the time goes in v1:
time: 28.2 us; the launch traced here: 27.7 us
  starting transfers between devices  12.6 us (45%)
  Pallas kernels  8.87 us (31%)
  local copies, waits for them, and re-layouts  2.42 us (9%)
  between operations  2.03 us (7%)
  waiting for transfers between devices  1.17 us (4%)
  other arithmetic  0.66 us (2%)
    all_to_all x1, starting transfers between devices, local(): everyone = lax.all_to_all(totals, AXES, 0, 0, tiled=True)  5.82 us
    pallas_call x1, Pallas kernels, local(): pl.pallas_call(main_kernel, out_shape=(jax.ShapeDtypeStruct((out_rows, CO...  4.86 us
    ppermute x1, starting transfers between devices, local(): got_tail = lax.ppermute(codes[rows - tail_rows:], AXES, next_two)  4.39 us
    ppermute x1, starting transfers between devices, local(): got_pack = lax.ppermute(pack, AXES, next_one)  2.39 us
    pallas_call x1, Pallas kernels, local(): pl.pallas_call(last_kernel, out_shape=jax.ShapeDtypeStruct((out_rows, COD...  2.02 us
    pallas_call x1, Pallas kernels, local(): pl.pallas_call(first_kernel, out_shape=(jax.ShapeDtypeStruct((devices, 1,...  1.99 us
    unnamed x10, local copies, waits for them, and re-layouts  1.83 us
    all_to_all x1, waiting for transfers between devices, local(): everyone = lax.all_to_all(totals, AXES, 0, 0, tiled=True)  1.16 us
  transfers between devices with their start and end apart: 3, of which 1 were waited for; matrix products, arithmetic and copies ran while one was open for 0% of the time, Pallas kernels for 18%

profile of v1, /device:TPU:0, one launch (start us, length us, event | category | flops | bytes accessed | tf_op | source)
XLA Modules:
  0.0 27.7 jit_solution(4310727021107262645)
XLA Ops:
  0.6 0.0 copy-start.2
  0.6 0.0 copy-start.1
  2.0 0.0 copy-done.2
  2.0 0.6 %reshape.20.ends = s32[1,768]{1,0:T(1,128)} reshape(s32[768]{0:T(1024)S(1)} %copy-done.2) | data formatting | bytes 6144 | tf_op jit(solution)/shard_map/reshape | solution.py:213
  2.6 0.7 %pad_add_fusion = (s32[2]{0:T(128)}, s32[2]{0:T(128)}) fusion(s32[1]{0:T(128)} %bitcast.1, s32[1]{0:T(128)} %bitcast, s32[1]{0:T(128)S(6)} %copy.7, s32[1]{0:T(128)S(6)} %copy.6), kind=kLoop, calls=%fused_computation.1 | loop fusion | flops 4 | bytes 32 | tf_op jit(solution)/shard_map/stack | solution.py:210
  3.2 2.0 %totals.1 = (f32[32,1,256]{2,1,0:T(1,128)}, s32[72,128]{1,0:T(8,128)}) custom-call(s32[2]{0:T(128)} %get-tuple-element.12.place, s32[2]{0:T(128)} %get-tuple-element.13.counts, s32[64,128]{1,0:T(8,128)} %bitcast.5, s32[1,768]{1,0:T(1,128)} %reshape.20.ends), custom_call_target="tpu_custom_call" | custom-call | tf_op jit(solution)/shard_map/totals/pallas_call | solution.py:217
  5.2 2.4 %collective-permute-start = (s32[72,128]{1,0:T(8,128)}, s32[72,128]{1,0:T(8,128)S(1)}, u32[]{:S(2)}, u32[]{:S(2)}) collective-permute-start(s32[72,128]{1,0:T(8,128)} %get-tuple-element.7), channel_id=1, source_target_pairs={{0,1},{1,2},{2,3},{3,4},{4,5},{5,6},{6,7},{7,8},{8,9},{9,10},{10,1... | collective-permute-start | bytes 110600 | tf_op jit(solution)/shard_map/ppermute | solution.py:231
  7.6 0.0 copy-done.1
  7.6 4.4 %collective-permute-start.1 = (s32[32,128]{1,0:T(8,128)S(1)}, s32[32,128]{1,0:T(8,128)S(1)}, u32[]{:S(2)}, u32[]{:S(2)}) collective-permute-start(s32[32,128]{1,0:T(8,128)S(1)} %slice_bitcast_fusion), channel_id=1, source_target_pairs={{0,2},{1,3},{2,4},{3,5},{4,6},{5,7},{6,8},{7,9},{8,10},{9,11},{10,... | collective-permute-start | bytes 49160 | tf_op jit(solution)/shard_map/ppermute | solution.py:232
  12.0 5.8 %all-to-all-start = ((f32[32,1,256]{2,1,0:T(1,128)}), f32[32,1,256]{2,1,0:T(1,128)S(1)}, u32[]{:S(2)}, u32[]{:S(2)}) async-start(f32[32,1,256]{2,1,0:T(1,128)} %get-tuple-element.9), calls=%async_computation | async-start | bytes 65536 | tf_op jit(solution)/shard_map/all_to_all | solution.py:228
  17.9 0.0 collective-permute-done.1.tail
  17.9 0.0 copy-start.4
  17.9 0.0 collective-permute-done.pack
  17.9 0.6 %copy-done.4 = s32[32,128]{1,0:T(8,128)} copy-done((s32[32,128]{1,0:T(8,128)}, s32[32,128]{1,0:T(8,128)S(1)}, u32[]{:S(2)}) %copy-start.4) | copy-done | bytes 16408
  18.5 0.0 copy-start.3
  18.5 0.6 %copy-done.3 = s32[72,128]{1,0:T(8,128)} copy-done((s32[72,128]{1,0:T(8,128)}, s32[72,128]{1,0:T(8,128)S(1)}, u32[]{:S(2)}) %copy-start.3) | copy-done | bytes 36888
  19.1 4.9 %windows.1 = (f32[512,256]{1,0:T(8,128)}, f32[512,256]{1,0:T(8,128)}, f32[512,128]{1,0:T(8,128)}) custom-call(s32[2]{0:T(128)} %get-tuple-element.12.place, s32[2]{0:T(128)} %get-tuple-element.13.counts, s32[64,128]{1,0:T(8,128)} %bitcast.6, s32[1,768]{1,0:T(1,128)} %reshape.20.ends, s32[72,128]{1,0:T(8,128)} %copy-done.3, s32[32,128]{1,0:T(8,128)} %copy-done.4), custom_call_target="tpu_custom_call" | custom-call | flops 713031680 | bytes 2097152 | tf_op jit(solution)/shard_map/windows/pallas_call | solution.py:237
  24.0 1.2 %all-to-all-done.totals = f32[32,1,256]{2,1,0:T(1,128)S(1)} async-done(((f32[32,1,256]{2,1,0:T(1,128)}), f32[32,1,256]{2,1,0:T(1,128)S(1)}, u32[]{:S(2)}, u32[]{:S(2)}) %all-to-all-start) | async-done | bytes 32800 | tf_op jit(solution)/shard_map/all_to_all | solution.py:228
  25.1 0.0 copy-start
  25.1 0.6 %copy-done = f32[32,1,256]{2,1,0:T(1,128)} copy-done((f32[32,1,256]{2,1,0:T(1,128)}, f32[32,1,256]{2,1,0:T(1,128)S(1)}, u32[]{:S(2)}) %copy-start) | copy-done | bytes 32792
  25.7 2.0 %gap.1 = f32[512,256]{1,0:T(8,128)} custom-call(s32[2]{0:T(128)} %get-tuple-element.12.place, f32[32,1,256]{2,1,0:T(1,128)} %copy-done, f32[512,256]{1,0:T(8,128)} %get-tuple-element.10.base, f32[512,128]{1,0:T(8,128)} %get-tuple-element.11.weight), custom_call_target="tpu_custom_call" | custom-call | tf_op jit(solution)/shard_map/gap/pallas_call | solution.py:258
  (1 shorter events, 0.0 us)
Async XLA Ops:
  0.6 1.3 %copy-start.2 = (s32[768]{0:T(1024)S(1)}, s32[768]{0:T(1024)}, u32[]{:S(2)}) copy-start(s32[768]{0:T(1024)} %param.5) | copy-start | bytes 9220
  0.6 7.0 %copy-start.1 = (s32[8192]{0:T(1024)S(1)}, s32[8192]{0:T(1024)}, u32[]{:S(2)}) copy-start(s32[8192]{0:T(1024)} %param.4) | copy-start | bytes 98308
  5.2 12.7 %collective-permute-start = (s32[72,128]{1,0:T(8,128)}, s32[72,128]{1,0:T(8,128)S(1)}, u32[]{:S(2)}, u32[]{:S(2)}) collective-permute-start(s32[72,128]{1,0:T(8,128)} %get-tuple-element.7), channel_id=1, source_target_pairs={{0,1},{1,2},{2,3},{3,4},{4,5},{5,6},{6,7},{7,8},{8,9},{9,10},{10,1... | collective-permute-start | bytes 110600 | tf_op jit(solution)/shard_map/ppermute | solution.py:231
  7.6 10.2 %collective-permute-start.1 = (s32[32,128]{1,0:T(8,128)S(1)}, s32[32,128]{1,0:T(8,128)S(1)}, u32[]{:S(2)}, u32[]{:S(2)}) collective-permute-start(s32[32,128]{1,0:T(8,128)S(1)} %slice_bitcast_fusion), channel_id=1, source_target_pairs={{0,2},{1,3},{2,4},{3,5},{4,6},{5,7},{6,8},{7,9},{8,10},{9,11},{10,... | collective-permute-start | bytes 49160 | tf_op jit(solution)/shard_map/ppermute | solution.py:232
  12.0 13.1 %all-to-all-start = ((f32[32,1,256]{2,1,0:T(1,128)}), f32[32,1,256]{2,1,0:T(1,128)S(1)}, u32[]{:S(2)}, u32[]{:S(2)}) async-start(f32[32,1,256]{2,1,0:T(1,128)} %get-tuple-element.9), calls=%async_computation | async-start | bytes 65536 | tf_op jit(solution)/shard_map/all_to_all | solution.py:228
  17.9 0.6 %copy-start.4 = (s32[32,128]{1,0:T(8,128)}, s32[32,128]{1,0:T(8,128)S(1)}, u32[]{:S(2)}) copy-start(s32[32,128]{1,0:T(8,128)S(1)} %collective-permute-done.1.tail) | copy-start | bytes 49156
  18.5 0.6 %copy-start.3 = (s32[72,128]{1,0:T(8,128)}, s32[72,128]{1,0:T(8,128)S(1)}, u32[]{:S(2)}) copy-start(s32[72,128]{1,0:T(8,128)S(1)} %collective-permute-done.pack) | copy-start | bytes 110596
  25.1 0.6 %copy-start = (f32[32,1,256]{2,1,0:T(1,128)}, f32[32,1,256]{2,1,0:T(1,128)S(1)}, u32[]{:S(2)}) copy-start(f32[32,1,256]{2,1,0:T(1,128)S(1)} %all-to-all-done.totals) | copy-start | bytes 98308

commit v2 on v1

v2 whole, which is shorter than its diff:
```python
import jax
import jax.numpy as jnp
from jax import lax
from jax.experimental import pallas as pl
from jax.experimental.pallas import tpu as pltpu
from jax.sharding import PartitionSpec as P


CODES = 256
WINDOW = 4096
LANES = 128
BLOCK = 16
PACK = 16
VMEM_LIMIT = 16 * 2**20
FIRST_LIMIT = 60 * 2**20
AXES = ("seq", "grp")
F32 = jnp.float32
BF16 = jnp.bfloat16


def label_groups():
    base = lax.broadcasted_iota(jnp.int32, (PACK, LANES), 0).astype(F32)
    return [(base + PACK * k).astype(BF16) for k in range(CODES // PACK)]


def tally_rows(rows, labels):
    total = [None] * len(labels)
    one, zero = jnp.ones((PACK, LANES), BF16), jnp.zeros((PACK, LANES), BF16)
    for row in rows:
        wide = jnp.broadcast_to(row, (PACK, LANES)).astype(BF16)
        for k, label in enumerate(labels):
            hit = jnp.where(wide == label, one, zero)
            total[k] = hit if total[k] is None else total[k] + hit
    return total


def lane_row(block):
    return jnp.concatenate([block[k : k + 1, :] for k in range(block.shape[0])], axis=1)


def shard_place():
    within = lax.axis_index("grp")
    return lax.axis_index("seq") * lax.axis_size("grp") + within, within


def first_kernel(codes, ends, out_totals, out_ends, tally):
    devices = out_totals.shape[0]
    rows = codes.shape[0]
    slot_rows = ends.shape[0]
    out_ends[:slot_rows, :] = ends[...]
    used = jnp.sum((ends[...] > 0).astype(jnp.int32), axis=(0, 1), keepdims=True)
    used = used + (ends[:1, :1] == 0).astype(jnp.int32)
    out_ends[slot_rows:, :] = jnp.broadcast_to(used, (1, LANES))
    values = codes[...]
    wide = values.astype(F32)
    groups = tally_rows([wide[r : r + 1, :] for r in range(rows)], label_groups())
    for k, group in enumerate(groups):
        tally[k * PACK : (k + 1) * PACK, :] = group
    total = lax.dot_general(
        jnp.ones((8, LANES), BF16),
        tally[...],
        (((1,), (1,)), ((), ())),
        preferred_element_type=F32,
    )
    out_totals[...] = jnp.broadcast_to(total[:1, :].reshape(1, 1, CODES), (devices, 1, CODES))


def block_tallies(left, source, count, labels):
    for g in range(count):
        found = tally_rows([source[g * BLOCK + i : g * BLOCK + i + 1, :] for i in range(BLOCK)], labels)
        for k, group in enumerate(found):
            left[k * PACK : (k + 1) * PACK, g * LANES : (g + 1) * LANES] = group


def block_kernel(codes, near, out_left, out_first, turned):
    shard = shard_place()[0]
    groups = LANES // BLOCK
    before = jnp.where(shard > 0, near[...], -1)
    turned[...] = jnp.concatenate([before, codes[...]], axis=0).astype(F32).T
    block_tallies(out_left, turned, groups, label_groups())
    for g in range(groups):
        here = turned[g * BLOCK : (g + 1) * BLOCK, :]
        if g + 1 < groups:
            after = turned[(g + 1) * BLOCK : (g + 2) * BLOCK, :]
        else:
            after = pltpu.roll(turned[:BLOCK, :], LANES - 1, axis=1)
        out_left[CODES:, g * LANES : (g + 1) * LANES] = (after - here).astype(BF16)
    out_first[...] = turned[:BLOCK, :]


def main_kernel(left, first, packed, relayed, out_share, out_base, out_weight,
                side, side_left, mask, parts):
    shard, within = shard_place()
    tail_rows = WINDOW // LANES
    slot_rows = packed.shape[0] - tail_rows - 2
    slots = slot_rows * LANES
    mine, tail, meta = packed.at[tail_rows:, :], relayed.at[:tail_rows, :], relayed.at[tail_rows:, :]
    rows = left.shape[1] * BLOCK // (2 * LANES)
    shard_len = rows * LANES
    out_rows = out_share.shape[0]
    groups = LANES // BLOCK
    side_blocks = side.shape[0] // BLOCK
    split = LANES // tail_rows
    labels = label_groups()

    far = jnp.where(shard > 1, tail[...], -1).astype(F32)
    step = LANES // split
    stacked = jnp.concatenate(
        [far] + [pltpu.roll(far, LANES - step * k, axis=1) for k in range(1, split)], axis=0
    )
    side[...] = stacked.T[:step, :]
    block_tallies(side_left, side, side_blocks, labels)
    lane = lax.broadcasted_iota(jnp.int32, (BLOCK, LANES), 1)
    for g in range(side_blocks):
        here = side[g * BLOCK : (g + 1) * BLOCK, :]
        if g + 1 < side_blocks:
            after = side[(g + 1) * BLOCK : (g + 2) * BLOCK, :]
        else:
            top = side[:BLOCK, :]
            after = jnp.where(
                lane < LANES - tail_rows,
                pltpu.roll(top, LANES - tail_rows, axis=1),
                pltpu.roll(top, LANES - tail_rows - 1, axis=1),
            )
            after = jnp.where(lane < LANES - 1, after, first[:, :1])
        side_left[CODES:, g * LANES : (g + 1) * LANES] = (after - here).astype(BF16)

    handed = jnp.max(meta[slot_rows + 1 :, :])
    given = jnp.max(meta[slot_rows : slot_rows + 1, :]) - handed
    arrived = jnp.where(within > 0, handed, 0)
    kept = mine[slot_rows : slot_rows + 1, :] - mine[slot_rows + 1 :, :]
    kept = jnp.concatenate([kept] * (out_rows // LANES), axis=1)

    def rolled(block, shift):
        wide = jnp.broadcast_to(lane_row(block[:slot_rows, :]), (8, slots))
        return pltpu.roll(wide, shift, axis=1)[:1, :out_rows]

    own = rolled(mine, arrived)
    sent = rolled(meta, lax.rem(slots - given, slots))
    row = lax.broadcasted_iota(jnp.int32, (1, out_rows), 1)
    end = jnp.where(row < arrived, sent - shard_len, own)
    valid = row < arrived + kept
    end = jnp.where(valid, end, 0)

    upper = end + 1 + shard_len
    lower = upper - WINDOW
    upper_block, lower_block = upper >> 4, lower >> 4
    down = lax.broadcasted_iota(jnp.int32, (PACK, out_rows), 0).astype(F32)
    downs = [(down + PACK * k).astype(BF16) for k in range(LANES // PACK)]
    one, zero = jnp.ones((PACK, out_rows), BF16), jnp.zeros((PACK, out_rows), BF16)

    def limit(value):
        bound = jnp.clip(value, 0, LANES).astype(F32)
        return jnp.broadcast_to(bound, (PACK, out_rows)).astype(BF16)

    for g in range(groups):
        high = limit((upper_block - g + groups - 1) >> 3)
        low = limit((lower_block - g + groups - 1) >> 3)
        for k in range(LANES // PACK):
            reach = jnp.where(downs[k] < high, one, zero)
            skip = jnp.where(downs[k] < low, one, zero)
            base = g * LANES + k * PACK
            mask[base : base + PACK, :out_rows] = reach - one if k * PACK < rows else reach
            mask[base : base + PACK, out_rows:] = reach - skip
    side_block = lower_block + tail_rows * groups
    for g in range(side_blocks):
        for part in range(split):
            low = limit((side_block - side_blocks * part - g + groups - 1) >> 3)
            for k in range(tail_rows // PACK):
                base = (groups + g) * LANES + part * tail_rows + k * PACK
                mask[base : base + PACK, out_rows:] = jnp.where(downs[k] < low, zero, one)

    main_depth = groups * LANES
    parts[:, :out_rows] = jnp.dot(
        left[...], mask[:main_depth, :out_rows], preferred_element_type=F32
    )
    parts[:, out_rows:] = jnp.dot(
        left[...], mask[:main_depth, out_rows:], preferred_element_type=F32
    ) + jnp.dot(side_left[...], mask[main_depth:, out_rows:], preferred_element_type=F32)

    upper_codes = parts[CODES:, :out_rows] + first[:, rows : rows + 1]
    lower_codes = upper_codes - parts[CODES:, out_rows:]
    inner = lax.broadcasted_iota(jnp.int32, (BLOCK, out_rows), 0)
    upper_codes = jnp.where(inner < (upper & (BLOCK - 1)), upper_codes, -2.0)
    lower_codes = jnp.where(inner < (lower & (BLOCK - 1)), lower_codes, -2.0)
    position = (shard * shard_len + end + 1).astype(F32)
    share_weight = jnp.where(valid, CODES / jnp.minimum(position, float(WINDOW)), 0.0)
    gap_weight = jnp.where(valid, CODES / position, 0.0)
    for q in range(out_rows // LANES):
        cut = slice(q * LANES, (q + 1) * LANES)
        ups = tally_rows([upper_codes[i : i + 1, cut] for i in range(BLOCK)], labels)
        lows = tally_rows([lower_codes[i : i + 1, cut] for i in range(BLOCK)], labels)
        lower_cut = slice(out_rows + q * LANES, out_rows + (q + 1) * LANES)
        shares, bases = [], []
        for k in range(CODES // PACK):
            span = slice(k * PACK, (k + 1) * PACK)
            up = ups[k].astype(F32)
            run = parts[span, cut] + up
            tally = parts[span, lower_cut] + (up - lows[k].astype(F32))
            share = tally * share_weight[:, cut]
            shares.append(share)
            bases.append(share - run * gap_weight[:, cut])
        out_share[cut, :] = jnp.concatenate(shares, axis=0).T
        out_base[cut, :] = jnp.concatenate(bases, axis=0).T
        out_weight[cut, :] = jnp.broadcast_to(gap_weight[:, cut], (LANES, LANES)).T


def last_kernel(totals, base, weight, out_gap):
    devices = totals.shape[0]
    shard = shard_place()[0]
    order = lax.broadcasted_iota(jnp.int32, (devices, 1, CODES), 0)
    offset = jnp.sum(jnp.where(order < shard, totals[...], 0.0), axis=0)
    for k in range(CODES // LANES):
        cut = slice(k * LANES, (k + 1) * LANES)
        out_gap[:, cut] = base[:, cut] - weight[...] * offset[:, cut]


def local(event_codes, window_ends, window_count, handed):
    group = lax.axis_size("grp")
    devices = lax.axis_size("seq") * group
    shard_len, slots = event_codes.shape[0], window_ends.shape[0]
    rows = shard_len // LANES
    tail_rows = WINDOW // LANES
    out_rows = 2 * slots // 3
    ends = window_ends.reshape(slots // LANES, LANES)
    vmem = pl.BlockSpec(memory_space=pltpu.VMEM)
    params = pltpu.CompilerParams(vmem_limit_bytes=VMEM_LIMIT)
    to_next = [(i, (i + 1) % devices) for i in range(devices)]
    in_group = [(i, (i + 1) % group) for i in range(group)]

    near = lax.ppermute(event_codes, AXES, to_next)
    codes = event_codes.reshape(rows, LANES)
    totals, held_ends = pl.pallas_call(
        first_kernel,
        out_shape=(
            jax.ShapeDtypeStruct((devices, 1, CODES), F32),
            jax.ShapeDtypeStruct((slots // LANES + 1, LANES), jnp.int32),
        ),
        in_specs=[vmem] * 2,
        out_specs=(vmem, vmem),
        scratch_shapes=[pltpu.VMEM((CODES, LANES), BF16)],
        compiler_params=pltpu.CompilerParams(vmem_limit_bytes=FIRST_LIMIT),
        name="totals",
    )(codes, ends)
    everyone = lax.all_to_all(totals, AXES, 0, 0, tiled=True)
    near = near.reshape(rows, LANES)
    passing = jnp.broadcast_to(handed[:, None], (1, LANES))
    packed = jnp.concatenate([near[rows - tail_rows :], held_ends, passing])
    relayed = lax.ppermute(packed, "grp", in_group)

    depth = 2 * shard_len // BLOCK
    side_depth = WINDOW // BLOCK
    left, first = pl.pallas_call(
        block_kernel,
        out_shape=(
            jax.ShapeDtypeStruct((CODES + BLOCK, depth), BF16),
            jax.ShapeDtypeStruct((BLOCK, LANES), F32),
        ),
        in_specs=[vmem, vmem],
        out_specs=(vmem, vmem),
        scratch_shapes=[pltpu.VMEM((LANES, LANES), F32)],
        compiler_params=params,
        cost_estimate=pl.CostEstimate(
            flops=2 * CODES * depth * LANES, bytes_accessed=2**20, transcendentals=0
        ),
        name="blocks",
    )(codes, near)
    share, base, weight = pl.pallas_call(
        main_kernel,
        out_shape=(
            jax.ShapeDtypeStruct((out_rows, CODES), F32),
            jax.ShapeDtypeStruct((out_rows, CODES), F32),
            jax.ShapeDtypeStruct((out_rows, LANES), F32),
        ),
        in_specs=[vmem] * 4,
        out_specs=(vmem, vmem, vmem),
        scratch_shapes=[
            pltpu.VMEM((tail_rows, LANES), F32),
            pltpu.VMEM((CODES + BLOCK, side_depth), BF16),
            pltpu.VMEM((depth + side_depth, 2 * out_rows), BF16),
            pltpu.VMEM((CODES + BLOCK, 2 * out_rows), F32),
        ],
        compiler_params=params,
        cost_estimate=pl.CostEstimate(
            flops=2 * (CODES + BLOCK) * depth * 2 * out_rows,
            bytes_accessed=2**21,
            transcendentals=0,
        ),
        name="windows",
    )(left, first, packed, relayed)
    gap = pl.pallas_call(
        last_kernel,
        out_shape=jax.ShapeDtypeStruct((out_rows, CODES), F32),
        in_specs=[vmem, vmem, vmem],
        out_specs=vmem,
        compiler_params=params,
        name="gap",
    )(everyone, base, weight)
    return share, gap


def solution(mesh):
    in_specs = (P(AXES), P(AXES), P(AXES), P(AXES))
    out_specs = (P(AXES, None), P(AXES, None))
    return jax.shard_map(local, mesh=mesh, in_specs=in_specs, out_specs=out_specs, check_vma=False)
```

time: 28.2 us -> 21.9 us (0.78)
  starting transfers between devices: 12.6 us -> 4.35 us
  waiting for transfers between devices: 1.17 us -> 8.11 us
  Pallas kernels: 8.87 us -> 7 us
  local copies, waits for them, and re-layouts: 2.42 us -> 0.77 us
  between operations: 2.03 us -> 1.33 us
  other arithmetic: 0.66 us -> 0.07 us
    ppermute x2, starting transfers between devices: 6.78 us -> 0.55 us  [the longest x1 0.54 us: local(): near = lax.ppermute(event_codes, AXES, to_next)]
    ppermute x2, waiting for transfers between devices: 0.01 us -> 5 us  [the longest x1 5 us: local(): near = lax.ppermute(event_codes, AXES, to_next)]
    all_to_all x1, starting transfers between devices: 5.82 us -> 3.8 us  [local(): everyone = lax.all_to_all(totals, AXES, 0, 0, tiled=True)]
    all_to_all x1, waiting for transfers between devices: 1.16 us -> 3.11 us  [local(): everyone = lax.all_to_all(totals, AXES, 0, 0, tiled=True)]
    pallas_call x1, Pallas kernels: 4.86 us -> 3.11 us  [local(): pl.pallas_call(main_kernel, out_shape=(jax.ShapeDtypeStruct((out_rows, CO...]
    unnamed x10 -> x4, local copies, waits for them, and re-layouts: 1.83 us -> 0.69 us
    pallas_call x1, Pallas kernels: 2.02 us -> 0.89 us  [local(): pl.pallas_call(last_kernel, out_shape=jax.ShapeDtypeStruct((out_rows, COD...]
    pallas_call x0 -> x1, Pallas kernels: none -> 1 us  [local(): pl.pallas_call(block_kernel, out_shape=(jax.ShapeDtypeStruct((CODES + BLO...]
  transfers between devices with their start and end apart: 3 -> 3, of which waited for: 1 -> 2; matrix products, arithmetic and copies ran while one was open for 0% -> 0% of each run, Pallas kernels for 18% -> 28%
where the time goes in v2:
time: 21.9 us; the launch traced here: 21.6 us
  waiting for transfers between devices  8.11 us (37%)
  Pallas kernels  7 us (32%)
  starting transfers between devices  4.35 us (20%)
  between operations  1.33 us (6%)
  local copies, waits for them, and re-layouts  0.77 us (4%)
    ppermute x1, waiting for transfers between devices, local(): near = lax.ppermute(event_codes, AXES, to_next)  5 us
    all_to_all x1, starting transfers between devices, local(): everyone = lax.all_to_all(totals, AXES, 0, 0, tiled=True)  3.8 us
    pallas_call x1, Pallas kernels, local(): pl.pallas_call(main_kernel, out_shape=(jax.ShapeDtypeStruct((out_rows, CO...  3.11 us
    all_to_all x1, waiting for transfers between devices, local(): everyone = lax.all_to_all(totals, AXES, 0, 0, tiled=True)  3.11 us
    pallas_call x1, Pallas kernels, local(): pl.pallas_call(first_kernel, out_shape=(jax.ShapeDtypeStruct((devices, 1,...  2 us
    pallas_call x1, Pallas kernels, local(): pl.pallas_call(block_kernel, out_shape=(jax.ShapeDtypeStruct((CODES + BLO...  1 us
    pallas_call x1, Pallas kernels, local(): pl.pallas_call(last_kernel, out_shape=jax.ShapeDtypeStruct((out_rows, COD...  0.89 us
    unnamed x4, local copies, waits for them, and re-layouts  0.69 us
  transfers between devices with their start and end apart: 3, of which 2 were waited for; matrix products, arithmetic and copies ran while one was open for 0% of the time, Pallas kernels for 28%

profile of v2, /device:TPU:0, one launch (start us, length us, event | category | flops | bytes accessed | tf_op | source)
XLA Modules:
  0.0 21.6 jit_solution(171989181793453657)
XLA Ops:
  0.6 0.5 %collective-permute-start = (s32[8192]{0:T(1024)}, s32[8192]{0:T(1024)S(1)}, u32[]{:S(2)}, u32[]{:S(2)}) collective-permute-start(s32[8192]{0:T(1024)} %param.4), channel_id=1, source_target_pairs={{0,1},{1,2},{2,3},{3,4},{4,5},{5,6},{6,7},{7,8},{8,9},{9,10},{10,1... | collective-permute-start | bytes 98312 | tf_op jit(solution)/shard_map/ppermute | solution.py:231
  1.8 0.1 pad.2.clone
  1.9 2.0 %totals.1 = (f32[32,1,256]{2,1,0:T(1,128)}, s32[7,128]{1,0:T(8,128)}) custom-call(s32[64,128]{1,0:T(8,128)} %bitcast.6, s32[6,128]{1,0:T(8,128)} %bitcast.9), custom_call_target="tpu_custom_call" | custom-call | tf_op jit(solution)/shard_map/totals/pallas_call | solution.py:233
  3.9 5.0 %collective-permute-done = s32[8192]{0:T(1024)S(1)} collective-permute-done((s32[8192]{0:T(1024)}, s32[8192]{0:T(1024)S(1)}, u32[]{:S(2)}, u32[]{:S(2)}) %collective-permute-start) | collective-permute-done | bytes 32800 | tf_op jit(solution)/shard_map/ppermute | solution.py:231
  8.9 0.0 copy-start.1
  8.9 0.7 %copy-done.1 = s32[7,128]{1,0:T(8,128)S(1)} copy-done((s32[7,128]{1,0:T(8,128)S(1)}, s32[7,128]{1,0:T(8,128)}, u32[]{:S(2)}) %copy-start.1) | copy-done | bytes 3608
  9.6 0.1 add_add_fusion.packed
  9.7 0.0 collective-permute-start.1
  9.7 0.0 copy-start
  9.7 3.8 %all-to-all-start = ((f32[32,1,256]{2,1,0:T(1,128)}), f32[32,1,256]{2,1,0:T(1,128)S(1)}, u32[]{:S(2)}, u32[]{:S(2)}) async-start(f32[32,1,256]{2,1,0:T(1,128)} %get-tuple-element.13), calls=%async_computation | async-start | bytes 65536 | tf_op jit(solution)/shard_map/all_to_all | solution.py:245
  13.5 0.0 copy-done
  13.5 1.0 %blocks.1 = (bf16[272,1024]{1,0:T(8,128)(2,1)S(1)}, f32[16,128]{1,0:T(8,128)S(1)}) custom-call(s32[64,128]{1,0:T(8,128)S(1)} %bitcast.7, s32[64,128]{1,0:T(8,128)S(1)} %bitcast.8), custom_call_target="tpu_custom_call" | custom-call | flops 67108864 | bytes 1048576 | tf_op jit(solution)/shard_map/blocks/pallas_call | solution.py:253
  14.5 0.0 collective-permute-done.1.relayed
  14.5 3.1 %windows.1 = (f32[512,256]{1,0:T(8,128)}, f32[512,256]{1,0:T(8,128)S(1)}, f32[512,128]{1,0:T(8,128)S(1)}) custom-call(bf16[272,1024]{1,0:T(8,128)(2,1)S(1)} %get-tuple-element.9.left, f32[16,128]{1,0:T(8,128)S(1)} %get-tuple-element.10.first, s32[40,128]{1,0:T(8,128)S(1)} %add_add_fusion.packed, s32[40,128]{1,0:T(8,128)S(1)} %collective-permute-done.1.relayed), custom_call_target="tpu_custom_call" | custom-call | flops 570425344 | bytes 2097152 | tf_op jit(solution)/shard_map/windows/pallas_call | solution.py:268
  17.6 3.1 %all-to-all-done.totals = f32[32,1,256]{2,1,0:T(1,128)S(1)} async-done(((f32[32,1,256]{2,1,0:T(1,128)}), f32[32,1,256]{2,1,0:T(1,128)S(1)}, u32[]{:S(2)}, u32[]{:S(2)}) %all-to-all-start) | async-done | bytes 32800 | tf_op jit(solution)/shard_map/all_to_all | solution.py:245
  20.7 0.9 %gap.1 = f32[512,256]{1,0:T(8,128)} custom-call(f32[32,1,256]{2,1,0:T(1,128)S(1)} %all-to-all-done.totals, f32[512,256]{1,0:T(8,128)S(1)} %get-tuple-element.14.base, f32[512,128]{1,0:T(8,128)S(1)} %get-tuple-element.15.weight), custom_call_target="tpu_custom_call" | custom-call | tf_op jit(solution)/shard_map/gap/pallas_call | solution.py:291
  (1 shorter events, 0.0 us)
Async XLA Ops:
  0.6 8.3 %collective-permute-start = (s32[8192]{0:T(1024)}, s32[8192]{0:T(1024)S(1)}, u32[]{:S(2)}, u32[]{:S(2)}) collective-permute-start(s32[8192]{0:T(1024)} %param.4), channel_id=1, source_target_pairs={{0,1},{1,2},{2,3},{3,4},{4,5},{5,6},{6,7},{7,8},{8,9},{9,10},{10,1... | collective-permute-start | bytes 98312 | tf_op jit(solution)/shard_map/ppermute | solution.py:231
  8.9 0.7 %copy-start.1 = (s32[7,128]{1,0:T(8,128)S(1)}, s32[7,128]{1,0:T(8,128)}, u32[]{:S(2)}) copy-start(s32[7,128]{1,0:T(8,128)} %get-tuple-element.11) | copy-start | bytes 10756
  9.7 4.8 %collective-permute-start.1 = (s32[40,128]{1,0:T(8,128)S(1)}, s32[40,128]{1,0:T(8,128)S(1)}, u32[]{:S(2)}, u32[]{:S(2)}) collective-permute-start(s32[40,128]{1,0:T(8,128)S(1)} %add_add_fusion.packed), channel_id=1, source_target_pairs={{0,1},{1,2},{2,3},{3,0},{4,5},{5,6},{6,7},{7,4},{8,9},{9,10},{10,1... | collective-permute-start | bytes 61448 | tf_op jit(solution)/shard_map/ppermute | solution.py:249
  9.7 3.8 %copy-start = (s32[8192]{0:T(1024)S(1)}, s32[8192]{0:T(1024)}, u32[]{:S(2)}) copy-start(s32[8192]{0:T(1024)} %param.4) | copy-start | bytes 98308
  9.7 11.1 %all-to-all-start = ((f32[32,1,256]{2,1,0:T(1,128)}), f32[32,1,256]{2,1,0:T(1,128)S(1)}, u32[]{:S(2)}, u32[]{:S(2)}) async-start(f32[32,1,256]{2,1,0:T(1,128)} %get-tuple-element.13), calls=%async_computation | async-start | bytes 65536 | tf_op jit(solution)/shard_map/all_to_all | solution.py:245

commit v3 on v2

--- a/solution.py
+++ b/solution.py
@@ -1,3 +1,5 @@
+import functools
+
 import jax
 import jax.numpy as jnp
 from jax import lax
@@ -12,7 +14,6 @@
 BLOCK = 16
 PACK = 16
 VMEM_LIMIT = 16 * 2**20
-FIRST_LIMIT = 60 * 2**20
 AXES = ("seq", "grp")
 F32 = jnp.float32
 BF16 = jnp.bfloat16
@@ -43,15 +44,9 @@
     return lax.axis_index("seq") * lax.axis_size("grp") + within, within
 
 
-def first_kernel(codes, ends, out_totals, out_ends, tally):
+def first_kernel(rows, base, out_totals, tally):
     devices = out_totals.shape[0]
-    rows = codes.shape[0]
-    slot_rows = ends.shape[0]
-    out_ends[:slot_rows, :] = ends[...]
-    used = jnp.sum((ends[...] > 0).astype(jnp.int32), axis=(0, 1), keepdims=True)
-    used = used + (ends[:1, :1] == 0).astype(jnp.int32)
-    out_ends[slot_rows:, :] = jnp.broadcast_to(used, (1, LANES))
-    values = codes[...]
+    values = base[:rows, :]
     wide = values.astype(F32)
     groups = tally_rows([wide[r : r + 1, :] for r in range(rows)], label_groups())
     for k, group in enumerate(groups):
@@ -72,11 +67,22 @@
             left[k * PACK : (k + 1) * PACK, g * LANES : (g + 1) * LANES] = group
 
 
-def block_kernel(codes, near, out_left, out_first, turned):
+def block_kernel(rows, base, near, out_left, out_first, out_bounds, out_count, turned):
     shard = shard_place()[0]
     groups = LANES // BLOCK
-    before = jnp.where(shard > 0, near[...], -1)
-    turned[...] = jnp.concatenate([before, codes[...]], axis=0).astype(F32).T
+    slots = out_bounds.shape[1]
+
+    def used(ends):
+        above = jnp.sum((ends > 0).astype(jnp.int32), axis=(0, 1), keepdims=True)
+        return above + (ends[:1, :1] == 0).astype(jnp.int32)
+
+    ends, prior_ends = base[rows:, :], near[rows:, :]
+    out_bounds[:1, :] = lane_row(ends)
+    wide = jnp.broadcast_to(lane_row(prior_ends), (8, slots))
+    out_bounds[1:, :] = pltpu.roll(wide, slots - jnp.max(used(prior_ends)), axis=1)[:1, :]
+    out_count[...] = jnp.broadcast_to(used(ends), (1, LANES))
+    before = jnp.where(shard > 0, near[:rows, :], -1)
+    turned[...] = jnp.concatenate([before, base[:rows, :]], axis=0).astype(F32).T
     block_tallies(out_left, turned, groups, label_groups())
     for g in range(groups):
         here = turned[g * BLOCK : (g + 1) * BLOCK, :]
@@ -88,13 +94,12 @@
     out_first[...] = turned[:BLOCK, :]
 
 
-def main_kernel(left, first, packed, relayed, out_share, out_base, out_weight,
+def main_kernel(left, first, bounds, count, handed, relayed, out_share, out_base, out_weight,
                 side, side_left, mask, parts):
     shard, within = shard_place()
-    tail_rows = WINDOW // LANES
-    slot_rows = packed.shape[0] - tail_rows - 2
-    slots = slot_rows * LANES
-    mine, tail, meta = packed.at[tail_rows:, :], relayed.at[:tail_rows, :], relayed.at[tail_rows:, :]
+    tail_rows = relayed.shape[0] - 1
+    tail = relayed.at[:tail_rows, :]
+    slots = bounds.shape[1]
     rows = left.shape[1] * BLOCK // (2 * LANES)
     shard_len = rows * LANES
     out_rows = out_share.shape[0]
@@ -125,18 +130,15 @@
             after = jnp.where(lane < LANES - 1, after, first[:, :1])
         side_left[CODES:, g * LANES : (g + 1) * LANES] = (after - here).astype(BF16)
 
-    handed = jnp.max(meta[slot_rows + 1 :, :])
-    given = jnp.max(meta[slot_rows : slot_rows + 1, :]) - handed
-    arrived = jnp.where(within > 0, handed, 0)
-    kept = mine[slot_rows : slot_rows + 1, :] - mine[slot_rows + 1 :, :]
-    kept = jnp.concatenate([kept] * (out_rows // LANES), axis=1)
-
-    def rolled(block, shift):
-        wide = jnp.broadcast_to(lane_row(block[:slot_rows, :]), (8, slots))
-        return pltpu.roll(wide, shift, axis=1)[:1, :out_rows]
-
-    own = rolled(mine, arrived)
-    sent = rolled(meta, lax.rem(slots - given, slots))
+    given = jnp.max(relayed[tail_rows:, :])
+    arrived = jnp.where(within > 0, given, 0)
+    kept = jnp.concatenate([count[...] - handed[...]] * (out_rows // LANES), axis=1)
+
+    def moved(row, shift):
+        return pltpu.roll(jnp.broadcast_to(row, (8, slots)), shift, axis=1)[:1, :out_rows]
+
+    own = moved(bounds[:1, :], arrived)
+    sent = moved(bounds[1:, :], given)
     row = lax.broadcasted_iota(jnp.int32, (1, out_rows), 1)
     end = jnp.where(row < arrived, sent - shard_len, own)
     valid = row < arrived + kept
@@ -205,14 +207,26 @@
         out_weight[cut, :] = jnp.broadcast_to(gap_weight[:, cut], (LANES, LANES)).T
 
 
-def last_kernel(totals, base, weight, out_gap):
+def last_kernel(totals, share, base, weight, out_share, out_gap, gap, sent):
     devices = totals.shape[0]
+    out_rows = share.shape[0]
+    shared = pltpu.make_async_copy(share, out_share, sent.at[0])
+    shared.start()
     shard = shard_place()[0]
     order = lax.broadcasted_iota(jnp.int32, (devices, 1, CODES), 0)
     offset = jnp.sum(jnp.where(order < shard, totals[...], 0.0), axis=0)
-    for k in range(CODES // LANES):
-        cut = slice(k * LANES, (k + 1) * LANES)
-        out_gap[:, cut] = base[:, cut] - weight[...] * offset[:, cut]
+    pieces = out_rows // LANES
+    copies = []
+    for p in range(pieces):
+        span = pl.ds(p * LANES, LANES)
+        for k in range(CODES // LANES):
+            cut = slice(k * LANES, (k + 1) * LANES)
+            gap[span, cut] = base[span, cut] - weight[span, :] * offset[:, cut]
+        copies.append(pltpu.make_async_copy(gap.at[span], out_gap.at[span], sent.at[1 + p]))
+        copies[-1].start()
+    shared.wait()
+    for copy in copies:
+        copy.wait()
 
 
 def local(event_codes, window_ends, window_count, handed):
@@ -222,57 +236,57 @@
     rows = shard_len // LANES
     tail_rows = WINDOW // LANES
     out_rows = 2 * slots // 3
-    ends = window_ends.reshape(slots // LANES, LANES)
+    hbm = pl.BlockSpec(memory_space=pltpu.HBM)
     vmem = pl.BlockSpec(memory_space=pltpu.VMEM)
     params = pltpu.CompilerParams(vmem_limit_bytes=VMEM_LIMIT)
     to_next = [(i, (i + 1) % devices) for i in range(devices)]
     in_group = [(i, (i + 1) % group) for i in range(group)]
 
-    near = lax.ppermute(event_codes, AXES, to_next)
-    codes = event_codes.reshape(rows, LANES)
-    totals, held_ends = pl.pallas_call(
-        first_kernel,
-        out_shape=(
-            jax.ShapeDtypeStruct((devices, 1, CODES), F32),
-            jax.ShapeDtypeStruct((slots // LANES + 1, LANES), jnp.int32),
-        ),
-        in_specs=[vmem] * 2,
-        out_specs=(vmem, vmem),
+    base = jnp.concatenate(
+        [event_codes.reshape(rows, LANES), window_ends.reshape(slots // LANES, LANES)]
+    )
+    near = lax.ppermute(base, AXES, to_next)
+    totals = pl.pallas_call(
+        functools.partial(first_kernel, rows),
+        out_shape=jax.ShapeDtypeStruct((devices, 1, CODES), F32),
+        in_specs=[vmem],
+        out_specs=vmem,
         scratch_shapes=[pltpu.VMEM((CODES, LANES), BF16)],
-        compiler_params=pltpu.CompilerParams(vmem_limit_bytes=FIRST_LIMIT),
+        compiler_params=params,
         name="totals",
-    )(codes, ends)
+    )(base)
     everyone = lax.all_to_all(totals, AXES, 0, 0, tiled=True)
-    near = near.reshape(rows, LANES)
     passing = jnp.broadcast_to(handed[:, None], (1, LANES))
-    packed = jnp.concatenate([near[rows - tail_rows :], held_ends, passing])
+    packed = jnp.concatenate([near[rows - tail_rows : rows], passing])
     relayed = lax.ppermute(packed, "grp", in_group)
 
     depth = 2 * shard_len // BLOCK
     side_depth = WINDOW // BLOCK
-    left, first = pl.pallas_call(
-        block_kernel,
+    left, first, bounds, count = pl.pallas_call(
+        functools.partial(block_kernel, rows),
         out_shape=(
             jax.ShapeDtypeStruct((CODES + BLOCK, depth), BF16),
             jax.ShapeDtypeStruct((BLOCK, LANES), F32),
+            jax.ShapeDtypeStruct((2, slots), jnp.int32),
+            jax.ShapeDtypeStruct((1, LANES), jnp.int32),
         ),
         in_specs=[vmem, vmem],
-        out_specs=(vmem, vmem),
+        out_specs=(vmem, vmem, vmem, vmem),
         scratch_shapes=[pltpu.VMEM((LANES, LANES), F32)],
         compiler_params=params,
         cost_estimate=pl.CostEstimate(
             flops=2 * CODES * depth * LANES, bytes_accessed=2**20, transcendentals=0
         ),
         name="blocks",
-    )(codes, near)
-    share, base, weight = pl.pallas_call(
+    )(base, near)
+    share, rest, weight = pl.pallas_call(
         main_kernel,
         out_shape=(
             jax.ShapeDtypeStruct((out_rows, CODES), F32),
             jax.ShapeDtypeStruct((out_rows, CODES), F32),
             jax.ShapeDtypeStruct((out_rows, LANES), F32),
         ),
-        in_specs=[vmem] * 4,
+        in_specs=[vmem] * 6,
         out_specs=(vmem, vmem, vmem),
         scratch_shapes=[
             pltpu.VMEM((tail_rows, LANES), F32),
@@ -287,15 +301,22 @@
             transcendentals=0,
         ),
         name="windows",
-    )(left, first, packed, relayed)
-    gap = pl.pallas_call(
+    )(left, first, bounds, count, passing, relayed)
+    share, gap = pl.pallas_call(
         last_kernel,
-        out_shape=jax.ShapeDtypeStruct((out_rows, CODES), F32),
-        in_specs=[vmem, vmem, vmem],
-        out_specs=vmem,
+        out_shape=(
+            jax.ShapeDtypeStruct((out_rows, CODES), F32),
+            jax.ShapeDtypeStruct((out_rows, CODES), F32),
+        ),
+        in_specs=[vmem] * 4,
+        out_specs=(hbm, hbm),
+        scratch_shapes=[
+            pltpu.VMEM((out_rows, CODES), F32),
+            pltpu.SemaphoreType.DMA((1 + out_rows // LANES,)),
+        ],
         compiler_params=params,
         name="gap",
-    )(everyone, base, weight)
+    )(everyone, share, rest, weight)
     return share, gap
 
 

time: 21.9 us -> 23 us (1.050)
  waiting for transfers between devices: 8.11 us -> 10.6 us
  Pallas kernels: 7 us -> 5.75 us
  local copies, waits for them, and re-layouts: 0.77 us -> 0.01 us
  other arithmetic: 0.07 us -> 0.78 us
    ppermute x1, waiting for transfers between devices: 5 us -> 6.9 us  [local(): near = lax.ppermute(base, AXES, to_next)]
    concatenate x1, other arithmetic: 0.07 us -> 0.78 us  [local(): jnp.concatenate([event_codes.reshape(rows, LANES), window_ends.reshape(sl...]
    unnamed x4 -> x0, local copies, waits for them, and re-layouts: 0.69 us -> none
    pallas_call x1, Pallas kernels: 3.11 us -> 2.49 us  [local(): pl.pallas_call(main_kernel, out_shape=(jax.ShapeDtypeStruct((out_rows, CO...]
    pallas_call x3, Pallas kernels: 3.88 us -> 3.26 us  [the longest x1 1.22 us: local(): pl.pallas_call(functools.partial(first_kernel, rows), out_shape=jax.Shape...]
    all_to_all x1, waiting for transfers between devices: 3.11 us -> 3.69 us  [local(): everyone = lax.all_to_all(totals, AXES, 0, 0, tiled=True)]
  transfers between devices with their start and end apart: 3 -> 3, of which waited for: 2 -> 2; matrix products, arithmetic and copies ran while one was open for 0% -> 0% of each run, Pallas kernels for 28% -> 21%
where the time goes in v3:
time: 23 us; the launch traced here: 22.8 us
  waiting for transfers between devices  10.6 us (46%)
  Pallas kernels  5.75 us (25%)
  starting transfers between devices  4.31 us (19%)
  between operations  1.32 us (6%)
  other arithmetic  0.78 us (3%)
    ppermute x1, waiting for transfers between devices, local(): near = lax.ppermute(base, AXES, to_next)  6.9 us
    all_to_all x1, starting transfers between devices, local(): everyone = lax.all_to_all(totals, AXES, 0, 0, tiled=True)  3.82 us
    all_to_all x1, waiting for transfers between devices, local(): everyone = lax.all_to_all(totals, AXES, 0, 0, tiled=True)  3.69 us
    pallas_call x1, Pallas kernels, local(): pl.pallas_call(main_kernel, out_shape=(jax.ShapeDtypeStruct((out_rows, CO...  2.49 us
    pallas_call x1, Pallas kernels, local(): pl.pallas_call(functools.partial(first_kernel, rows), out_shape=jax.Shape...  1.22 us
    pallas_call x1, Pallas kernels, local(): pl.pallas_call(functools.partial(block_kernel, rows), out_shape=(jax.Shap...  1.05 us
    pallas_call x1, Pallas kernels, local(): pl.pallas_call(last_kernel, out_shape=(jax.ShapeDtypeStruct((out_rows, CO...  1 us
    concatenate x1, other arithmetic, local(): jnp.concatenate([event_codes.reshape(rows, LANES), window_ends.reshape(sl...  0.78 us
  transfers between devices with their start and end apart: 3, of which 2 were waited for; matrix products, arithmetic and copies ran while one was open for 0% of the time, Pallas kernels for 21%

profile of v3, /device:TPU:0, one launch (start us, length us, event | category | flops | bytes accessed | tf_op | source)
XLA Modules:
  0.0 22.8 jit_solution(16948578340142829158)
XLA Ops:
  0.6 0.8 %pad_add_fusion.base = s32[70,128]{1,0:T(8,128)S(1)} fusion(s32[6,128]{1,0:T(8,128)} %bitcast.6, s32[64,128]{1,0:T(8,128)} %bitcast.5), kind=kLoop, calls=%fused_computation | loop fusion | flops 8960 | bytes 71680 | tf_op jit(solution)/shard_map/concatenate | solution.py:245
  1.4 0.5 %collective-permute-start = (s32[70,128]{1,0:T(8,128)S(1)}, s32[70,128]{1,0:T(8,128)S(1)}, u32[]{:S(2)}, u32[]{:S(2)}) collective-permute-start(s32[70,128]{1,0:T(8,128)S(1)} %pad_add_fusion.base), channel_id=1, source_target_pairs={{0,1},{1,2},{2,3},{3,4},{4,5},{5,6},{6,7},{7,8},{8,9},{9,10},{10,1... | collective-permute-start | bytes 107528 | tf_op jit(solution)/shard_map/ppermute | solution.py:248
  2.6 6.9 %collective-permute-done.near = s32[70,128]{1,0:T(8,128)S(1)} collective-permute-done((s32[70,128]{1,0:T(8,128)S(1)}, s32[70,128]{1,0:T(8,128)S(1)}, u32[]{:S(2)}, u32[]{:S(2)}) %collective-permute-start) | collective-permute-done | bytes 35872 | tf_op jit(solution)/shard_map/ppermute | solution.py:248
  9.5 0.0 collective-permute-start.1
  9.5 1.2 %totals.1 = f32[32,1,256]{2,1,0:T(1,128)} custom-call(s32[70,128]{1,0:T(8,128)S(1)} %pad_add_fusion.base), custom_call_target="tpu_custom_call" | custom-call | tf_op jit(solution)/shard_map/totals/pallas_call | solution.py:249
  10.7 3.8 %all-to-all-start = ((f32[32,1,256]{2,1,0:T(1,128)}), f32[32,1,256]{2,1,0:T(1,128)S(1)}, u32[]{:S(2)}, u32[]{:S(2)}) async-start(f32[32,1,256]{2,1,0:T(1,128)} %totals.1), calls=%async_computation | async-start | bytes 65536 | tf_op jit(solution)/shard_map/all_to_all | solution.py:258
  14.5 1.0 %blocks.1 = (bf16[272,1024]{1,0:T(8,128)(2,1)S(1)}, f32[16,128]{1,0:T(8,128)S(1)}, s32[2,768]{1,0:T(2,128)S(1)}, s32[1,128]{1,0:T(1,128)S(1)}) custom-call(s32[70,128]{1,0:T(8,128)S(1)} %pad_add_fusion.base, s32[70,128]{1,0:T(8,128)S(1)} %collective-permute-done.near), custom_call_target="tpu_custom_call" | custom-call | flops 67108864 | bytes 1048576 | tf_op jit(solution)/shard_map/blocks/pallas_call | solution.py:265
  15.6 0.0 collective-permute-done.1.relayed
  15.6 2.5 %windows.1 = (f32[512,256]{1,0:T(8,128)S(1)}, f32[512,256]{1,0:T(8,128)S(1)}, f32[512,128]{1,0:T(8,128)S(1)}) custom-call(bf16[272,1024]{1,0:T(8,128)(2,1)S(1)} %get-tuple-element.9.left, f32[16,128]{1,0:T(8,128)S(1)} %get-tuple-element.10.first, s32[2,768]{1,0:T(2,128)S(1)} %get-tuple-element.11.bounds, s32[1,128]{1,0:T(1,128)S(1)} %get-tuple-element.12.count, ...), custom_call_target="tpu_custom_call" | custom-call | flops 570425344 | bytes 2097152 | tf_op jit(solution)/shard_map/windows/pallas_call | solution.py:282
  18.1 3.7 %all-to-all-done.totals = f32[32,1,256]{2,1,0:T(1,128)S(1)} async-done(((f32[32,1,256]{2,1,0:T(1,128)}), f32[32,1,256]{2,1,0:T(1,128)S(1)}, u32[]{:S(2)}, u32[]{:S(2)}) %all-to-all-start) | async-done | bytes 32800 | tf_op jit(solution)/shard_map/all_to_all | solution.py:258
  21.8 1.0 %gap.1 = (f32[512,256]{1,0:T(8,128)}, f32[512,256]{1,0:T(8,128)}) custom-call(f32[32,1,256]{2,1,0:T(1,128)S(1)} %all-to-all-done.totals, f32[512,256]{1,0:T(8,128)S(1)} %get-tuple-element.13.share, f32[512,256]{1,0:T(8,128)S(1)} %get-tuple-element.14.base, f32[512,128]{1,0:T(8,128)S(1)} %get-tuple-element.15.weight), custom_call_target="tpu_custom_call" | custom-call | tf_op jit(solution)/shard_map/gap/pallas_call | solution.py:305
  (3 shorter events, 0.0 us)
Async XLA Ops:
  1.4 8.0 %collective-permute-start = (s32[70,128]{1,0:T(8,128)S(1)}, s32[70,128]{1,0:T(8,128)S(1)}, u32[]{:S(2)}, u32[]{:S(2)}) collective-permute-start(s32[70,128]{1,0:T(8,128)S(1)} %pad_add_fusion.base), channel_id=1, source_target_pairs={{0,1},{1,2},{2,3},{3,4},{4,5},{5,6},{6,7},{7,8},{8,9},{9,10},{10,1... | collective-permute-start | bytes 107528 | tf_op jit(solution)/shard_map/ppermute | solution.py:248
  9.5 6.1 %collective-permute-start.1 = (s32[33,128]{1,0:T(8,128)S(1)}, s32[33,128]{1,0:T(8,128)S(1)}, u32[]{:S(2)}, u32[]{:S(2)}) collective-permute-start(s32[33,128]{1,0:T(8,128)S(1)} %concatenate.7), channel_id=1, source_target_pairs={{0,1},{1,2},{2,3},{3,0},{4,5},{5,6},{6,7},{7,4},{8,9},{9,10},{10,1... | collective-permute-start | bytes 50696 | tf_op jit(solution)/shard_map/ppermute | solution.py:261
  10.7 11.1 %all-to-all-start = ((f32[32,1,256]{2,1,0:T(1,128)}), f32[32,1,256]{2,1,0:T(1,128)S(1)}, u32[]{:S(2)}, u32[]{:S(2)}) async-start(f32[32,1,256]{2,1,0:T(1,128)} %totals.1), calls=%async_computation | async-start | bytes 65536 | tf_op jit(solution)/shard_map/all_to_all | solution.py:258

commit v4 on v3

--- a/solution.py
+++ b/solution.py
@@ -44,20 +44,31 @@
     return lax.axis_index("seq") * lax.axis_size("grp") + within, within
 
 
-def first_kernel(rows, base, out_totals, tally):
+def first_kernel(rows, base, out_totals):
     devices = out_totals.shape[0]
     values = base[:rows, :]
-    wide = values.astype(F32)
-    groups = tally_rows([wide[r : r + 1, :] for r in range(rows)], label_groups())
-    for k, group in enumerate(groups):
-        tally[k * PACK : (k + 1) * PACK, :] = group
-    total = lax.dot_general(
-        jnp.ones((8, LANES), BF16),
-        tally[...],
+    half = CODES // PACK
+    labels = lax.broadcasted_iota(jnp.int32, (PACK, LANES), 0).astype(F32).astype(BF16)
+    one, zero = jnp.ones((PACK, LANES), BF16), jnp.zeros((PACK, LANES), BF16)
+    highs, lows = [], []
+    for part, hits in (((values >> 4).astype(F32), highs), ((values & (half - 1)).astype(F32), lows)):
+        for r in range(rows):
+            wide = jnp.broadcast_to(part[r : r + 1, :], (PACK, LANES)).astype(BF16)
+            hits.append(jnp.where(wide == labels, one, zero))
+    pair = lax.dot_general(
+        jnp.concatenate(highs, axis=1),
+        jnp.concatenate(lows, axis=1),
         (((1,), (1,)), ((), ())),
         preferred_element_type=F32,
     )
-    out_totals[...] = jnp.broadcast_to(total[:1, :].reshape(1, 1, CODES), (devices, 1, CODES))
+    spread = jnp.concatenate([pair, jnp.zeros((PACK, LANES - half), F32)], axis=1)
+    lines = []
+    for k in range(CODES // LANES):
+        step = LANES // half
+        turn = pltpu.roll(spread[k * step : (k + 1) * step, :], 0, axis=1, stride=half, stride_axis=0)
+        lines.append(jnp.sum(turn, axis=0, keepdims=True))
+    total = jnp.concatenate(lines, axis=1)
+    out_totals[...] = jnp.broadcast_to(total.reshape(1, 1, CODES), (devices, 1, CODES))
 
 
 def block_tallies(left, source, count, labels):
@@ -95,14 +106,14 @@
 
 
 def main_kernel(left, first, bounds, count, handed, relayed, out_share, out_base, out_weight,
-                side, side_left, mask, parts):
+                side, side_left, mask, parts, share_rows, leave):
     shard, within = shard_place()
     tail_rows = relayed.shape[0] - 1
     tail = relayed.at[:tail_rows, :]
     slots = bounds.shape[1]
     rows = left.shape[1] * BLOCK // (2 * LANES)
     shard_len = rows * LANES
-    out_rows = out_share.shape[0]
+    out_rows = out_base.shape[0]
     groups = LANES // BLOCK
     side_blocks = side.shape[0] // BLOCK
     split = LANES // tail_rows
@@ -188,6 +199,7 @@
     position = (shard * shard_len + end + 1).astype(F32)
     share_weight = jnp.where(valid, CODES / jnp.minimum(position, float(WINDOW)), 0.0)
     gap_weight = jnp.where(valid, CODES / position, 0.0)
+    copies = []
     for q in range(out_rows // LANES):
         cut = slice(q * LANES, (q + 1) * LANES)
         ups = tally_rows([upper_codes[i : i + 1, cut] for i in range(BLOCK)], labels)
@@ -202,16 +214,18 @@
             share = tally * share_weight[:, cut]
             shares.append(share)
             bases.append(share - run * gap_weight[:, cut])
-        out_share[cut, :] = jnp.concatenate(shares, axis=0).T
+        share_rows[cut, :] = jnp.concatenate(shares, axis=0).T
+        copies.append(pltpu.make_async_copy(share_rows.at[cut], out_share.at[cut], leave.at[q]))
+        copies[-1].start()
         out_base[cut, :] = jnp.concatenate(bases, axis=0).T
         out_weight[cut, :] = jnp.broadcast_to(gap_weight[:, cut], (LANES, LANES)).T
-
-
-def last_kernel(totals, share, base, weight, out_share, out_gap, gap, sent):
+    for copy in copies:
+        copy.wait()
+
+
+def last_kernel(totals, base, weight, out_gap, gap, sent):
     devices = totals.shape[0]
-    out_rows = share.shape[0]
-    shared = pltpu.make_async_copy(share, out_share, sent.at[0])
-    shared.start()
+    out_rows = base.shape[0]
     shard = shard_place()[0]
     order = lax.broadcasted_iota(jnp.int32, (devices, 1, CODES), 0)
     offset = jnp.sum(jnp.where(order < shard, totals[...], 0.0), axis=0)
@@ -222,9 +236,8 @@
         for k in range(CODES // LANES):
             cut = slice(k * LANES, (k + 1) * LANES)
             gap[span, cut] = base[span, cut] - weight[span, :] * offset[:, cut]
-        copies.append(pltpu.make_async_copy(gap.at[span], out_gap.at[span], sent.at[1 + p]))
+        copies.append(pltpu.make_async_copy(gap.at[span], out_gap.at[span], sent.at[p]))
         copies[-1].start()
-    shared.wait()
     for copy in copies:
         copy.wait()
 
@@ -251,7 +264,6 @@
         out_shape=jax.ShapeDtypeStruct((devices, 1, CODES), F32),
         in_specs=[vmem],
         out_specs=vmem,
-        scratch_shapes=[pltpu.VMEM((CODES, LANES), BF16)],
         compiler_params=params,
         name="totals",
     )(base)
@@ -287,12 +299,14 @@
             jax.ShapeDtypeStruct((out_rows, LANES), F32),
         ),
         in_specs=[vmem] * 6,
-        out_specs=(vmem, vmem, vmem),
+        out_specs=(hbm, vmem, vmem),
         scratch_shapes=[
             pltpu.VMEM((tail_rows, LANES), F32),
             pltpu.VMEM((CODES + BLOCK, side_depth), BF16),
             pltpu.VMEM((depth + side_depth, 2 * out_rows), BF16),
             pltpu.VMEM((CODES + BLOCK, 2 * out_rows), F32),
+            pltpu.VMEM((out_rows, CODES), F32),
+            pltpu.SemaphoreType.DMA((out_rows // LANES,)),
         ],
         compiler_params=params,
         cost_estimate=pl.CostEstimate(
@@ -302,21 +316,18 @@
         ),
         name="windows",
     )(left, first, bounds, count, passing, relayed)
-    share, gap = pl.pallas_call(
+    gap = pl.pallas_call(
         last_kernel,
-        out_shape=(
-            jax.ShapeDtypeStruct((out_rows, CODES), F32),
-            jax.ShapeDtypeStruct((out_rows, CODES), F32),
-        ),
-        in_specs=[vmem] * 4,
-        out_specs=(hbm, hbm),
+        out_shape=jax.ShapeDtypeStruct((out_rows, CODES), F32),
+        in_specs=[vmem] * 3,
+        out_specs=hbm,
         scratch_shapes=[
             pltpu.VMEM((out_rows, CODES), F32),
-            pltpu.SemaphoreType.DMA((1 + out_rows // LANES,)),
+            pltpu.SemaphoreType.DMA((out_rows // LANES,)),
         ],
         compiler_params=params,
         name="gap",
-    )(everyone, share, rest, weight)
+    )(everyone, rest, weight)
     return share, gap
 
 

time: 23 us -> 22.6 us (0.983)
  waiting for transfers between devices: 10.6 us -> 10 us
    all_to_all x1, waiting for transfers between devices: 3.69 us -> 3.14 us  [local(): everyone = lax.all_to_all(totals, AXES, 0, 0, tiled=True)]
    pallas_call x1, Pallas kernels: 2.49 us -> 3.03 us  [local(): pl.pallas_call(main_kernel, out_shape=(jax.ShapeDtypeStruct((out_rows, CO...]
    pallas_call x1, Pallas kernels: 1.22 us -> 0.94 us  [local(): pl.pallas_call(functools.partial(first_kernel, rows), out_shape=jax.Shape...]
  transfers between devices with their start and end apart: 3 -> 3, of which waited for: 2 -> 2; matrix products, arithmetic and copies ran while one was open for 0% -> 0% of each run, Pallas kernels for 21% -> 22%
where the time goes in v4:
time: 22.6 us; the launch traced here: 22.4 us
  waiting for transfers between devices  10 us (44%)
  Pallas kernels  5.91 us (26%)
  starting transfers between devices  4.31 us (19%)
  between operations  1.33 us (6%)
  other arithmetic  0.78 us (3%)
    ppermute x1, waiting for transfers between devices, local(): near = lax.ppermute(base, AXES, to_next)  6.9 us
    all_to_all x1, starting transfers between devices, local(): everyone = lax.all_to_all(totals, AXES, 0, 0, tiled=True)  3.82 us
    all_to_all x1, waiting for transfers between devices, local(): everyone = lax.all_to_all(totals, AXES, 0, 0, tiled=True)  3.14 us
    pallas_call x1, Pallas kernels, local(): pl.pallas_call(main_kernel, out_shape=(jax.ShapeDtypeStruct((out_rows, CO...  3.03 us
    pallas_call x1, Pallas kernels, local(): pl.pallas_call(functools.partial(block_kernel, rows), out_shape=(jax.Shap...  1.05 us
    pallas_call x1, Pallas kernels, local(): pl.pallas_call(functools.partial(first_kernel, rows), out_shape=jax.Shape...  0.94 us
    pallas_call x1, Pallas kernels, local(): pl.pallas_call(last_kernel, out_shape=jax.ShapeDtypeStruct((out_rows, COD...  0.89 us
    concatenate x1, other arithmetic, local(): jnp.concatenate([event_codes.reshape(rows, LANES), window_ends.reshape(sl...  0.78 us
  transfers between devices with their start and end apart: 3, of which 2 were waited for; matrix products, arithmetic and copies ran while one was open for 0% of the time, Pallas kernels for 22%

profile of v4, /device:TPU:0, one launch (start us, length us, event | category | flops | bytes accessed | tf_op | source)
XLA Modules:
  0.0 22.4 jit_solution(6835271348195082822)
XLA Ops:
  0.6 0.8 %pad_add_fusion.base = s32[70,128]{1,0:T(8,128)S(1)} fusion(s32[6,128]{1,0:T(8,128)} %bitcast.6, s32[64,128]{1,0:T(8,128)} %bitcast.5), kind=kLoop, calls=%fused_computation | loop fusion | flops 8960 | bytes 71680 | tf_op jit(solution)/shard_map/concatenate | solution.py:258
  1.4 0.5 %collective-permute-start = (s32[70,128]{1,0:T(8,128)S(1)}, s32[70,128]{1,0:T(8,128)S(1)}, u32[]{:S(2)}, u32[]{:S(2)}) collective-permute-start(s32[70,128]{1,0:T(8,128)S(1)} %pad_add_fusion.base), channel_id=1, source_target_pairs={{0,1},{1,2},{2,3},{3,4},{4,5},{5,6},{6,7},{7,8},{8,9},{9,10},{10,1... | collective-permute-start | bytes 107528 | tf_op jit(solution)/shard_map/ppermute | solution.py:261
  2.6 6.9 %collective-permute-done.near = s32[70,128]{1,0:T(8,128)S(1)} collective-permute-done((s32[70,128]{1,0:T(8,128)S(1)}, s32[70,128]{1,0:T(8,128)S(1)}, u32[]{:S(2)}, u32[]{:S(2)}) %collective-permute-start) | collective-permute-done | bytes 35872 | tf_op jit(solution)/shard_map/ppermute | solution.py:261
  9.5 0.0 collective-permute-start.1
  9.5 0.9 %totals.1 = f32[32,1,256]{2,1,0:T(1,128)} custom-call(s32[70,128]{1,0:T(8,128)S(1)} %pad_add_fusion.base), custom_call_target="tpu_custom_call" | custom-call | tf_op jit(solution)/shard_map/totals/pallas_call | solution.py:262
  10.4 3.8 %all-to-all-start = ((f32[32,1,256]{2,1,0:T(1,128)}), f32[32,1,256]{2,1,0:T(1,128)S(1)}, u32[]{:S(2)}, u32[]{:S(2)}) async-start(f32[32,1,256]{2,1,0:T(1,128)} %totals.1), calls=%async_computation | async-start | bytes 65536 | tf_op jit(solution)/shard_map/all_to_all | solution.py:270
  14.2 1.0 %blocks.1 = (bf16[272,1024]{1,0:T(8,128)(2,1)S(1)}, f32[16,128]{1,0:T(8,128)S(1)}, s32[2,768]{1,0:T(2,128)S(1)}, s32[1,128]{1,0:T(1,128)S(1)}) custom-call(s32[70,128]{1,0:T(8,128)S(1)} %pad_add_fusion.base, s32[70,128]{1,0:T(8,128)S(1)} %collective-permute-done.near), custom_call_target="tpu_custom_call" | custom-call | flops 67108864 | bytes 1048576 | tf_op jit(solution)/shard_map/blocks/pallas_call | solution.py:277
  15.3 0.0 collective-permute-done.1.relayed
  15.3 3.0 %windows.1 = (f32[512,256]{1,0:T(8,128)}, f32[512,256]{1,0:T(8,128)S(1)}, f32[512,128]{1,0:T(8,128)S(1)}) custom-call(bf16[272,1024]{1,0:T(8,128)(2,1)S(1)} %get-tuple-element.9.left, f32[16,128]{1,0:T(8,128)S(1)} %get-tuple-element.10.first, s32[2,768]{1,0:T(2,128)S(1)} %get-tuple-element.11.bounds, s32[1,128]{1,0:T(1,128)S(1)} %get-tuple-element.12.count, ...), custom_call_target="tpu_custom_call" | custom-call | flops 570425344 | bytes 2097152 | tf_op jit(solution)/shard_map/windows/pallas_call | solution.py:294
  18.3 3.1 %all-to-all-done.totals = f32[32,1,256]{2,1,0:T(1,128)S(1)} async-done(((f32[32,1,256]{2,1,0:T(1,128)}), f32[32,1,256]{2,1,0:T(1,128)S(1)}, u32[]{:S(2)}, u32[]{:S(2)}) %all-to-all-start) | async-done | bytes 32800 | tf_op jit(solution)/shard_map/all_to_all | solution.py:270
  21.5 0.9 %gap.1 = f32[512,256]{1,0:T(8,128)} custom-call(f32[32,1,256]{2,1,0:T(1,128)S(1)} %all-to-all-done.totals, f32[512,256]{1,0:T(8,128)S(1)} %get-tuple-element.14.base, f32[512,128]{1,0:T(8,128)S(1)} %get-tuple-element.15.weight), custom_call_target="tpu_custom_call" | custom-call | tf_op jit(solution)/shard_map/gap/pallas_call | solution.py:319
  (3 shorter events, 0.0 us)
Async XLA Ops:
  1.4 8.0 %collective-permute-start = (s32[70,128]{1,0:T(8,128)S(1)}, s32[70,128]{1,0:T(8,128)S(1)}, u32[]{:S(2)}, u32[]{:S(2)}) collective-permute-start(s32[70,128]{1,0:T(8,128)S(1)} %pad_add_fusion.base), channel_id=1, source_target_pairs={{0,1},{1,2},{2,3},{3,4},{4,5},{5,6},{6,7},{7,8},{8,9},{9,10},{10,1... | collective-permute-start | bytes 107528 | tf_op jit(solution)/shard_map/ppermute | solution.py:261
  9.5 5.8 %collective-permute-start.1 = (s32[33,128]{1,0:T(8,128)S(1)}, s32[33,128]{1,0:T(8,128)S(1)}, u32[]{:S(2)}, u32[]{:S(2)}) collective-permute-start(s32[33,128]{1,0:T(8,128)S(1)} %concatenate.7), channel_id=1, source_target_pairs={{0,1},{1,2},{2,3},{3,0},{4,5},{5,6},{6,7},{7,4},{8,9},{9,10},{10,1... | collective-permute-start | bytes 50696 | tf_op jit(solution)/shard_map/ppermute | solution.py:273
  10.4 11.1 %all-to-all-start = ((f32[32,1,256]{2,1,0:T(1,128)}), f32[32,1,256]{2,1,0:T(1,128)S(1)}, u32[]{:S(2)}, u32[]{:S(2)}) async-start(f32[32,1,256]{2,1,0:T(1,128)} %totals.1), calls=%async_computation | async-start | bytes 65536 | tf_op jit(solution)/shard_map/all_to_all | solution.py:270

commit v5 on v4

--- a/solution.py
+++ b/solution.py
@@ -105,15 +105,15 @@
     out_first[...] = turned[:BLOCK, :]
 
 
-def main_kernel(left, first, bounds, count, handed, relayed, out_share, out_base, out_weight,
-                side, side_left, mask, parts, share_rows, leave):
+def main_kernel(left, first, bounds, count, handed, relayed, out_share, share_rows, out_run, out_weight,
+                side, side_left, mask, parts, leave):
     shard, within = shard_place()
     tail_rows = relayed.shape[0] - 1
     tail = relayed.at[:tail_rows, :]
     slots = bounds.shape[1]
     rows = left.shape[1] * BLOCK // (2 * LANES)
     shard_len = rows * LANES
-    out_rows = out_base.shape[0]
+    out_rows = out_run.shape[0]
     groups = LANES // BLOCK
     side_blocks = side.shape[0] // BLOCK
     split = LANES // tail_rows
@@ -205,37 +205,34 @@
         ups = tally_rows([upper_codes[i : i + 1, cut] for i in range(BLOCK)], labels)
         lows = tally_rows([lower_codes[i : i + 1, cut] for i in range(BLOCK)], labels)
         lower_cut = slice(out_rows + q * LANES, out_rows + (q + 1) * LANES)
-        shares, bases = [], []
+        shares, runs = [], []
         for k in range(CODES // PACK):
             span = slice(k * PACK, (k + 1) * PACK)
             up = ups[k].astype(F32)
-            run = parts[span, cut] + up
+            runs.append(parts[span, cut] + up)
             tally = parts[span, lower_cut] + (up - lows[k].astype(F32))
-            share = tally * share_weight[:, cut]
-            shares.append(share)
-            bases.append(share - run * gap_weight[:, cut])
+            shares.append(tally * share_weight[:, cut])
         share_rows[cut, :] = jnp.concatenate(shares, axis=0).T
         copies.append(pltpu.make_async_copy(share_rows.at[cut], out_share.at[cut], leave.at[q]))
         copies[-1].start()
-        out_base[cut, :] = jnp.concatenate(bases, axis=0).T
+        out_run[cut, :] = jnp.concatenate(runs, axis=0).T
         out_weight[cut, :] = jnp.broadcast_to(gap_weight[:, cut], (LANES, LANES)).T
     for copy in copies:
         copy.wait()
 
 
-def last_kernel(totals, base, weight, out_gap, gap, sent):
-    devices = totals.shape[0]
-    out_rows = base.shape[0]
+def last_kernel(totals, share, run, weight, out_gap, gap, sent):
+    out_rows = share.shape[0]
     shard = shard_place()[0]
-    order = lax.broadcasted_iota(jnp.int32, (devices, 1, CODES), 0)
-    offset = jnp.sum(jnp.where(order < shard, totals[...], 0.0), axis=0)
+    offset = lax.fori_loop(0, shard, lambda j, before: before + totals[j], jnp.zeros((1, CODES), F32))
     pieces = out_rows // LANES
     copies = []
     for p in range(pieces):
         span = pl.ds(p * LANES, LANES)
         for k in range(CODES // LANES):
             cut = slice(k * LANES, (k + 1) * LANES)
-            gap[span, cut] = base[span, cut] - weight[span, :] * offset[:, cut]
+            running = run[span, cut] + offset[:, cut]
+            gap[span, cut] = share[span, cut] - running * weight[span, :]
         copies.append(pltpu.make_async_copy(gap.at[span], out_gap.at[span], sent.at[p]))
         copies[-1].start()
     for copy in copies:
@@ -291,21 +288,21 @@
         ),
         name="blocks",
     )(base, near)
-    share, rest, weight = pl.pallas_call(
+    share, near_share, run, weight = pl.pallas_call(
         main_kernel,
         out_shape=(
+            jax.ShapeDtypeStruct((out_rows, CODES), F32),
             jax.ShapeDtypeStruct((out_rows, CODES), F32),
             jax.ShapeDtypeStruct((out_rows, CODES), F32),
             jax.ShapeDtypeStruct((out_rows, LANES), F32),
         ),
         in_specs=[vmem] * 6,
-        out_specs=(hbm, vmem, vmem),
+        out_specs=(hbm, vmem, vmem, vmem),
         scratch_shapes=[
             pltpu.VMEM((tail_rows, LANES), F32),
             pltpu.VMEM((CODES + BLOCK, side_depth), BF16),
             pltpu.VMEM((depth + side_depth, 2 * out_rows), BF16),
             pltpu.VMEM((CODES + BLOCK, 2 * out_rows), F32),
-            pltpu.VMEM((out_rows, CODES), F32),
             pltpu.SemaphoreType.DMA((out_rows // LANES,)),
         ],
         compiler_params=params,
@@ -319,7 +316,7 @@
     gap = pl.pallas_call(
         last_kernel,
         out_shape=jax.ShapeDtypeStruct((out_rows, CODES), F32),
-        in_specs=[vmem] * 3,
+        in_specs=[vmem] * 4,
         out_specs=hbm,
         scratch_shapes=[
             pltpu.VMEM((out_rows, CODES), F32),
@@ -327,7 +324,7 @@
         ],
         compiler_params=params,
         name="gap",
-    )(everyone, rest, weight)
+    )(everyone, near_share, run, weight)
     return share, gap
 
 

time: 22.6 us -> 22.6 us (level)
  no operation moved by 1% of the time
where the time goes in v5:
time: 22.6 us; the launch traced here: 22.3 us
  waiting for transfers between devices  10.1 us (45%)
  Pallas kernels  5.79 us (26%)
  starting transfers between devices  4.31 us (19%)
  between operations  1.33 us (6%)
  other arithmetic  0.78 us (3%)
    ppermute x1, waiting for transfers between devices, local(): near = lax.ppermute(base, AXES, to_next)  6.9 us
    all_to_all x1, starting transfers between devices, local(): everyone = lax.all_to_all(totals, AXES, 0, 0, tiled=True)  3.82 us
    all_to_all x1, waiting for transfers between devices, local(): everyone = lax.all_to_all(totals, AXES, 0, 0, tiled=True)  3.21 us
    pallas_call x1, Pallas kernels, local(): pl.pallas_call(main_kernel, out_shape=(jax.ShapeDtypeStruct((out_rows, CO...  2.96 us
    pallas_call x1, Pallas kernels, local(): pl.pallas_call(functools.partial(block_kernel, rows), out_shape=(jax.Shap...  1.05 us
    pallas_call x1, Pallas kernels, local(): pl.pallas_call(functools.partial(first_kernel, rows), out_shape=jax.Shape...  0.94 us
    pallas_call x1, Pallas kernels, local(): pl.pallas_call(last_kernel, out_shape=jax.ShapeDtypeStruct((out_rows, COD...  0.84 us
    concatenate x1, other arithmetic, local(): jnp.concatenate([event_codes.reshape(rows, LANES), window_ends.reshape(sl...  0.78 us
  transfers between devices with their start and end apart: 3, of which 2 were waited for; matrix products, arithmetic and copies ran while one was open for 0% of the time, Pallas kernels for 22%

profile of v5, /device:TPU:0, one launch (start us, length us, event | category | flops | bytes accessed | tf_op | source)
XLA Modules:
  0.0 22.3 jit_solution(1617376428189467052)
XLA Ops:
  0.6 0.8 %pad_add_fusion.base = s32[70,128]{1,0:T(8,128)S(1)} fusion(s32[6,128]{1,0:T(8,128)} %bitcast.6, s32[64,128]{1,0:T(8,128)} %bitcast.5), kind=kLoop, calls=%fused_computation | loop fusion | flops 8960 | bytes 71680 | tf_op jit(solution)/shard_map/concatenate | solution.py:255
  1.4 0.5 %collective-permute-start = (s32[70,128]{1,0:T(8,128)S(1)}, s32[70,128]{1,0:T(8,128)S(1)}, u32[]{:S(2)}, u32[]{:S(2)}) collective-permute-start(s32[70,128]{1,0:T(8,128)S(1)} %pad_add_fusion.base), channel_id=1, source_target_pairs={{0,1},{1,2},{2,3},{3,4},{4,5},{5,6},{6,7},{7,8},{8,9},{9,10},{10,1... | collective-permute-start | bytes 107528 | tf_op jit(solution)/shard_map/ppermute | solution.py:258
  2.6 6.9 %collective-permute-done.near = s32[70,128]{1,0:T(8,128)S(1)} collective-permute-done((s32[70,128]{1,0:T(8,128)S(1)}, s32[70,128]{1,0:T(8,128)S(1)}, u32[]{:S(2)}, u32[]{:S(2)}) %collective-permute-start) | collective-permute-done | bytes 35872 | tf_op jit(solution)/shard_map/ppermute | solution.py:258
  9.5 0.0 collective-permute-start.1
  9.5 0.9 %totals.1 = f32[32,1,256]{2,1,0:T(1,128)} custom-call(s32[70,128]{1,0:T(8,128)S(1)} %pad_add_fusion.base), custom_call_target="tpu_custom_call" | custom-call | tf_op jit(solution)/shard_map/totals/pallas_call | solution.py:259
  10.4 3.8 %all-to-all-start = ((f32[32,1,256]{2,1,0:T(1,128)}), f32[32,1,256]{2,1,0:T(1,128)S(1)}, u32[]{:S(2)}, u32[]{:S(2)}) async-start(f32[32,1,256]{2,1,0:T(1,128)} %totals.1), calls=%async_computation | async-start | bytes 65536 | tf_op jit(solution)/shard_map/all_to_all | solution.py:267
  14.2 1.0 %blocks.1 = (bf16[272,1024]{1,0:T(8,128)(2,1)S(1)}, f32[16,128]{1,0:T(8,128)S(1)}, s32[2,768]{1,0:T(2,128)S(1)}, s32[1,128]{1,0:T(1,128)S(1)}) custom-call(s32[70,128]{1,0:T(8,128)S(1)} %pad_add_fusion.base, s32[70,128]{1,0:T(8,128)S(1)} %collective-permute-done.near), custom_call_target="tpu_custom_call" | custom-call | flops 67108864 | bytes 1048576 | tf_op jit(solution)/shard_map/blocks/pallas_call | solution.py:274
  15.3 0.0 collective-permute-done.1.relayed
  15.3 3.0 %windows.1 = (f32[512,256]{1,0:T(8,128)}, f32[512,256]{1,0:T(8,128)S(1)}, f32[512,256]{1,0:T(8,128)S(1)}, f32[512,128]{1,0:T(8,128)S(1)}) custom-call(bf16[272,1024]{1,0:T(8,128)(2,1)S(1)} %get-tuple-element.10.left, f32[16,128]{1,0:T(8,128)S(1)} %get-tuple-element.11.first, s32[2,768]{1,0:T(2,128)S(1)} %get-tuple-element.12.bounds, ...), custom_call_target="tpu_custom_call" | custom-call | flops 570425344 | bytes 2097152 | tf_op jit(solution)/shard_map/windows/pallas_call | solution.py:291
  18.3 3.2 %all-to-all-done.totals = f32[32,1,256]{2,1,0:T(1,128)S(1)} async-done(((f32[32,1,256]{2,1,0:T(1,128)}), f32[32,1,256]{2,1,0:T(1,128)S(1)}, u32[]{:S(2)}, u32[]{:S(2)}) %all-to-all-start) | async-done | bytes 32800 | tf_op jit(solution)/shard_map/all_to_all | solution.py:267
  21.5 0.8 %gap.1 = f32[512,256]{1,0:T(8,128)} custom-call(f32[32,1,256]{2,1,0:T(1,128)S(1)} %all-to-all-done.totals, f32[512,256]{1,0:T(8,128)S(1)} %get-tuple-element.15.share, f32[512,256]{1,0:T(8,128)S(1)} %get-tuple-element.16.run, f32[512,128]{1,0:T(8,128)S(1)} %get-tuple-element.17.weight), custom_call_target="tpu_custom_call" | custom-call | tf_op jit(solution)/shard_map/gap/pallas_call | solution.py:316
  (3 shorter events, 0.0 us)
Async XLA Ops:
  1.4 8.0 %collective-permute-start = (s32[70,128]{1,0:T(8,128)S(1)}, s32[70,128]{1,0:T(8,128)S(1)}, u32[]{:S(2)}, u32[]{:S(2)}) collective-permute-start(s32[70,128]{1,0:T(8,128)S(1)} %pad_add_fusion.base), channel_id=1, source_target_pairs={{0,1},{1,2},{2,3},{3,4},{4,5},{5,6},{6,7},{7,8},{8,9},{9,10},{10,1... | collective-permute-start | bytes 107528 | tf_op jit(solution)/shard_map/ppermute | solution.py:258
  9.5 5.8 %collective-permute-start.1 = (s32[33,128]{1,0:T(8,128)S(1)}, s32[33,128]{1,0:T(8,128)S(1)}, u32[]{:S(2)}, u32[]{:S(2)}) collective-permute-start(s32[33,128]{1,0:T(8,128)S(1)} %concatenate.7), channel_id=1, source_target_pairs={{0,1},{1,2},{2,3},{3,0},{4,5},{5,6},{6,7},{7,4},{8,9},{9,10},{10,1... | collective-permute-start | bytes 50696 | tf_op jit(solution)/shard_map/ppermute | solution.py:270
  10.4 11.1 %all-to-all-start = ((f32[32,1,256]{2,1,0:T(1,128)}), f32[32,1,256]{2,1,0:T(1,128)S(1)}, u32[]{:S(2)}, u32[]{:S(2)}) async-start(f32[32,1,256]{2,1,0:T(1,128)} %totals.1), calls=%async_computation | async-start | bytes 65536 | tf_op jit(solution)/shard_map/all_to_all | solution.py:267
